TPU v7x, 128 devices: a whole 4x4x4 slice. The times are simulated.
128 devices in a mesh: gx: 4 (over x), gy: 4 (over z), gz: 8 (over y, core).
Axes of the slice: x: 4, y: 4, z: 4, core: 2. Of those that a mesh axis runs over, the one named last changes fastest.
Arguments:
- right_side: float32 [3, 32, 128, 1024], P(None, 'gx', 'gy', 'gz'), may hold values from -6 to 6
- mass_coef: float32 [3, 32, 128, 1024], P(None, 'gx', 'gy', 'gz'), may hold values from 0.3 to 3
- curl_coef: float32 [3, 32, 128, 1024], P(None, 'gx', 'gy', 'gz'), may hold values from 0.5 to 5
Outputs:
- solution: float32 [3, 32, 128, 1024], P(None, 'gx', 'gy', 'gz')
- residual: float32 [3, 32, 128, 1024], P(None, 'gx', 'gy', 'gz')
All inputs are finite; a program needn't handle non-finite values.
Results may differ from a plain program's by a relative error of at most 0.0003.
Values sent between devices are 32-bit elements; how exact they have to be, the bound alone decides.
A program may use at most 64 MiB of HBM per device.

v0:
```python
import functools
import jax
import jax.numpy as jnp
from jax import lax
from jax.experimental import pallas as pl
from jax.experimental.pallas import tpu as pltpu
from jax.sharding import PartitionSpec as P

ITERS = 4
THETA = 1.25
SIGMA = 1.25
MESH = pl.DeviceIdType.MESH
F32 = jnp.float32
NB = 8
ROWS = 32
LANES = 128
BASE = 8

ROUND = (
    (1, 0, 0),
    (-1, 0, 0),
    (0, 1, 0),
    (0, -1, 0),
    (0, 0, 1),
    (0, 0, -1),
    (1, -1, 0),
    (-1, 1, 0),
    (1, 0, -1),
    (-1, 0, 1),
    (0, 1, -1),
    (0, -1, 1),
)


def lane_id(rows=ROWS):
    return lax.broadcasted_iota(jnp.int32, (rows, LANES), 1)


def row_id(rows=ROWS):
    return lax.broadcasted_iota(jnp.int32, (rows, LANES), 0)


def roll(v, amount, axis):
    amount = amount % v.shape[axis]
    return v if amount == 0 else pltpu.roll(v, amount, axis)


def place(field, plane):
    return 16 * field + 2 * plane


def packed(acc, v, field, plane):
    at = place(field, plane)
    return jnp.where((lane_id() >> 1) == at // 2, roll(v, at - 127, 1), acc)


def below_y(v, row):
    return jnp.where(row_id() == 0, row, roll(v, 1, 0))


def below_z(v, slab, at):
    return jnp.where(lane_id() == 0, roll(slab, -at, 1), roll(v, 1, 1))


def above_z(v, slab, at):
    return jnp.where(lane_id() == 127, roll(slab, 127 - at, 1), roll(v, -1, 1))


def fold(v):
    return v[0:8] + v[8:16] + v[16:24] + v[24:32]


def cheb_coefficients(nu):
    zero = jnp.zeros_like(nu[0])

    def gram(i, j):
        return 0.5 * (nu[i + j] + nu[abs(i - j)])

    def applied(c):
        out = [zero] * (len(c) + 1)
        for i, a in enumerate(c):
            if i == 0:
                out[1] = out[1] + a
            else:
                out[i + 1] = out[i + 1] + 0.5 * a
                out[i - 1] = out[i - 1] + 0.5 * a
        out = [SIGMA * a for a in out]
        for i, a in enumerate(c):
            out[i] = out[i] + THETA * a
        return out

    def dot(c, d):
        total = zero
        for i, a in enumerate(c):
            for j, b in enumerate(d):
                total = total + a * b * gram(i, j)
        return total

    res = [zero + 1.0]
    direction = None
    iterate = [zero] * ITERS
    gamma_old = alpha_old = None
    for iteration in range(ITERS):
        gamma = dot(res, res)
        delta = dot(applied(res), res)
        if iteration == 0:
            alpha = gamma / delta
            direction = list(res)
        else:
            beta = gamma / gamma_old
            alpha = gamma / (delta - beta * gamma / alpha_old)
            direction = [
                a + (beta * direction[i] if i < len(direction) else zero) for i, a in enumerate(res)
            ]
        for i, a in enumerate(direction):
            iterate[i] = iterate[i] + alpha * a
        image = applied(direction)
        res = [(res[i] if i < len(res) else zero) - alpha * a for i, a in enumerate(image)]
        gamma_old, alpha_old = gamma, alpha
    return iterate, res


def kernel(
    sizes,
    r_hbm,
    m_hbm,
    k_hbm,
    x_out,
    res_out,
    V,
    M,
    K,
    ID,
    IDN,
    F,
    U,
    CX,
    CYS,
    CY,
    CZS,
    CZ,
    YS,
    YR,
    ZS,
    ZR,
    YZR,
    MOM,
    RA,
    SB,
    RB,
    XO,
    RO,
    load_sem,
    c_send,
    c_recv,
    n_send,
    n_recv,
    a_send,
    a_recv,
):
    nx, ny, nz = sizes
    gx, gy, gz = lax.axis_index("gx"), lax.axis_index("gy"), lax.axis_index("gz")

    def device(dx, dy, dz):
        return {
            "gx": lax.rem(gx + dx + nx, nx),
            "gy": lax.rem(gy + dy + ny, ny),
            "gz": lax.rem(gz + dz + nz, nz),
        }

    def remote(src, dst, send, recv, offset):
        return pltpu.make_async_remote_copy(
            src_ref=src,
            dst_ref=dst,
            send_sem=send,
            recv_sem=recv,
            device_id=device(*offset),
            device_id_type=MESH,
        )

    loads = [
        pltpu.make_async_copy(k_hbm, K, load_sem.at[0]),
        pltpu.make_async_copy(m_hbm, M, load_sem.at[1]),
        pltpu.make_async_copy(r_hbm, V.at[0], load_sem.at[2]),
    ]
    for c in loads:
        c.start()
    barrier = pltpu.get_barrier_semaphore()
    for o in ROUND:
        pl.semaphore_signal(barrier, inc=1, device_id=device(*o), device_id_type=MESH)
    for c in loads:
        c.wait()
    y_fields = (K.at[0], K.at[2], M.at[1], V.at[0, 1])
    z_fields = (K.at[0], K.at[1], M.at[2], V.at[0, 2])
    for f, ref in enumerate(y_fields):
        for i in range(NB):
            CYS[f, i : i + 1, :] = ref[i, 31:32, :]
    slab = jnp.zeros((ROWS, LANES), F32)
    for f, ref in enumerate(z_fields):
        for i in range(NB):
            slab = packed(slab, ref[i], f, i)
    CZS[...] = slab
    pl.semaphore_wait(barrier, len(ROUND))
    coef = [
        remote(K.at[1:3, NB - 1], CX.at[0:2], c_send.at[0], c_recv.at[0], (1, 0, 0)),
        remote(M.at[0, NB - 1], CX.at[2], c_send.at[1], c_recv.at[1], (1, 0, 0)),
        remote(V.at[0, 0, NB - 1], CX.at[3], c_send.at[2], c_recv.at[2], (1, 0, 0)),
        remote(CYS, CY, c_send.at[3], c_recv.at[3], (0, 1, 0)),
        remote(CZS, CZ, c_send.at[4], c_recv.at[4], (0, 0, 1)),
    ]
    for c in coef:
        c.start()
    for c in coef:
        c.wait()

    def finish(j, i, slab, values):
        for f, v in enumerate(values):
            F[j, f, 1 + i, BASE : BASE + ROWS, :] = v
            YS[j, f, i : i + 1, :] = v[31:32]
            if f != 1:
                YS[j, (4, 0, 5, 6)[f], i : i + 1, :] = v[0:1]
            slab = packed(slab, v, f, i)
        return slab

    slab = jnp.zeros((ROWS, LANES), F32)
    cz = CZ[...]
    k1_lo, k2_lo, m0_lo, r0_lo = CX[0], CX[1], CX[2], CX[3]
    for i in range(NB):
        k0, k1, k2 = K[0, i], K[1, i], K[2, i]
        m0, m1, m2 = M[0, i], M[1, i], M[2, i]
        r0, r1, r2 = V[0, 0, i], V[0, 1, i], V[0, 2, i]
        k0y = below_y(k0, CY[0, i : i + 1, :])
        k2y = below_y(k2, CY[1, i : i + 1, :])
        m1y = below_y(m1, CY[2, i : i + 1, :])
        r1y = below_y(r1, CY[3, i : i + 1, :])
        k0z = below_z(k0, cz, place(0, i))
        k1z = below_z(k1, cz, place(1, i))
        m2z = below_z(m2, cz, place(2, i))
        r2z = below_z(r2, cz, place(3, i))
        id0 = 1.0 / (m0 + k1 + k1z + k2 + k2y)
        id1 = 1.0 / (m1 + k2 + k2_lo + k0 + k0z)
        id2 = 1.0 / (m2 + k0 + k0y + k1 + k1_lo)
        idn = 1.0 / (m0 + m0_lo + m1 + m1y + m2 + m2z)
        phi = idn * ((r0_lo - r0) + (r1y - r1) + (r2z - r2))
        ID[0, i], ID[1, i], ID[2, i], IDN[i] = id0, id1, id2, idn
        slab = finish(0, i, slab, (r0 * id0, r1 * id1, r2 * id2, phi))
        k1_lo, k2_lo, m0_lo, r0_lo = k1, k2, m0, r0
    ZS[0] = slab

    def messages(j):
        pairs = (
            (F.at[j, 0:4, NB, BASE : BASE + ROWS], F.at[j, 0:4, 0, BASE : BASE + ROWS]),
            (F.at[j, 1:4, 1, BASE : BASE + ROWS], F.at[j, 1:4, NB + 1, BASE : BASE + ROWS]),
            (YS.at[j, 0:4], YR.at[j, 0:4]),
            (YS.at[j, 4:7], YR.at[j, 4:7]),
            (ZS.at[j], ZR.at[j, 0]),
            (ZS.at[j], ZR.at[j, 1]),
            (YS.at[j, 4], YR.at[j, 7]),
            (YS.at[j, 1], YR.at[j, 8]),
            (ZS.at[j], ZR.at[j, 2]),
            (ZS.at[j], ZR.at[j, 3]),
            (ZS.at[j, 24:32], YZR.at[j, 0]),
            (ZS.at[j, 0:8], YZR.at[j, 1]),
        )
        return [
            remote(src, dst, n_send.at[j, k], n_recv.at[j, k], ROUND[k])
            for k, (src, dst) in enumerate(pairs)
        ]

    def one_round(j, carry):
        copies = messages(j)
        for c in copies:
            c.start()
        for c in copies:
            c.wait()
        first = j == 0
        scale = jnp.where(first, F32(1.0 / SIGMA), F32(2.0 / SIGMA))
        back = jnp.where(first, F32(0.0), F32(1.0))
        before = jnp.maximum(j - 1, 0)
        for f, at in ((0, 4), (2, 5), (3, 6)):
            for i in range(NB):
                F[j, f, 1 + i, BASE + ROWS : BASE + ROWS + 1, :] = YR[j, at, i : i + 1, :]
        F[j, 0, 0, BASE + ROWS : BASE + ROWS + 1, :] = YR[j, 7, 7:8, :]
        sub, lane8 = row_id(8), lane_id(8)
        s0, s1, s2, ph = YR[j, 0], YR[j, 1], YR[j, 2], YR[j, 3]
        own0, own2, own_ph = YS[j, 4], YS[j, 5], YS[j, 6]
        s1x = jnp.where(sub == 7, YR[j, 8, 0:1, :], roll(s1, -1, 0))
        corner = jnp.where(lane8 == place(1, sub) + 1, YZR[j, 0, 7:8, :], 0.0)
        corner = jnp.sum(corner, axis=1, keepdims=True)
        s1z = jnp.where(lane8 == 127, corner, roll(s1, -1, 1))
        CYS[0] = CY[0] * ((own2 - s2) - (s1z - s1))
        CYS[1] = CY[1] * ((s1x - s1) - (own0 - s0))
        CYS[2] = CY[2] * (s1 + (own_ph - ph))
        lane, row = lane_id(), row_id()
        low = jnp.where((lane & 1) == 1, ZS[j], ZR[j, 0])
        cz = CZ[...]
        z0, z1 = low, roll(low, -16, 1)
        z2, zp = roll(low, -32, 1), roll(low, -48, 1)
        z2y = jnp.where(row == 31, roll(YZR[j, 1, 0:8, :], -32, 1)[0:1], roll(z2, -1, 0))
        z2x = jnp.where(lane == 14, roll(ZR[j, 3], 14 - 32, 1), roll(z2, -2, 1))
        gz0 = cz * ((z2y - z2) - (roll(z1, -1, 1) - z1))
        gz1 = roll(cz, -16, 1) * ((roll(z0, -1, 1) - z0) - (z2x - z2))
        mz2 = roll(cz, -32, 1) * (z2 + (roll(zp, -1, 1) - zp))
        high = ZR[j, 1]

        def field(f, i):
            return F[j, f, 1 + i, BASE : BASE + ROWS, :]

        def above_y(f, i):
            return F[j, f, 1 + i, BASE + 1 : BASE + 1 + ROWS, :]

        e0, e1, e2, ph = field(0, -1), field(1, -1), field(2, -1), field(3, -1)
        n0, n1, n2, nph = field(0, 0), field(1, 0), field(2, 0), field(3, 0)
        e0z = above_z(e0, ZR[j, 2], place(0, 7) + 1)
        g1_lo = CX[0] * ((e0z - e0) - (n2 - e2))
        g2_lo = CX[1] * ((n1 - e1) - (above_y(0, -1) - e0))
        f0_lo = CX[2] * (e0 + (nph - ph))
        slab = jnp.zeros((ROWS, LANES), F32)
        uv = jnp.zeros((8, LANES), F32)
        wu = jnp.zeros((8, LANES), F32)
        for i in range(NB):
            e0, e1, e2, ph = n0, n1, n2, nph
            if i < NB - 1:
                n0 = field(0, i + 1)
            n1, n2, nph = field(1, i + 1), field(2, i + 1), field(3, i + 1)
            e0z = above_z(e0, high, place(0, i) + 1)
            e1z = above_z(e1, high, place(1, i) + 1)
            phz = above_z(ph, high, place(3, i) + 1)
            g0 = K[0, i] * ((above_y(2, i) - e2) - (e1z - e1))
            g1 = K[1, i] * ((e0z - e0) - (n2 - e2))
            g2 = K[2, i] * ((n1 - e1) - (above_y(0, i) - e0))
            d0, d1, d2 = nph - ph, above_y(3, i) - ph, phz - ph
            u0, u1, u2 = e0 + d0, e1 + d1, e2 + d2
            m0, m1, m2 = M[0, i], M[1, i], M[2, i]
            f0, f1, f2 = m0 * u0, m1 * u1, m2 * u2
            g0y = below_y(g0, CYS[0, i : i + 1, :])
            g2y = below_y(g2, CYS[1, i : i + 1, :])
            f1y = below_y(f1, CYS[2, i : i + 1, :])
            g0z = below_z(g0, gz0, 2 * i)
            g1z = below_z(g1, gz1, 2 * i)
            f2z = below_z(f2, mz2, 2 * i)
            w0 = (g1z - g1) - (g2y - g2) + f0
            w1 = (g2_lo - g2) - (g0z - g0) + f1
            w2 = (g0y - g0) - (g1_lo - g1) + f2
            q = IDN[i] * ((f0_lo - f0) + (f1y - f1) + (f2z - f2))
            v0, v1, v2 = V[j, 0, i], V[j, 1, i], V[j, 2, i]
            U[j, 0, i], U[j, 1, i], U[j, 2, i] = u0, u1, u2
            w0 = scale * (w0 - THETA * v0) - back * V[before, 0, i]
            w1 = scale * (w1 - THETA * v1) - back * V[before, 1, i]
            w2 = scale * (w2 - THETA * v2) - back * V[before, 2, i]
            q = scale * (q - THETA * ph) - back * F[before, 3, 1 + i, BASE : BASE + ROWS, :]
            V[j + 1, 0, i], V[j + 1, 1, i], V[j + 1, 2, i] = w0, w1, w2
            uv = uv + fold(v0 * u0 + v1 * u1 + v2 * u2)
            wu = wu + fold(w0 * u0 + w1 * u1 + w2 * u2)
            slab = finish(j + 1, i, slab, (w0 * ID[0, i], w1 * ID[1, i], w2 * ID[2, i], q))
            g1_lo, g2_lo, f0_lo = g1, g2, f0
        ZS[j + 1] = slab
        MOM[pl.ds(2 * j, 1), :] = jnp.sum(uv, axis=0, keepdims=True)
        MOM[pl.ds(2 * j + 1, 1), :] = jnp.sum(wu, axis=0, keepdims=True)
        return carry

    lax.fori_loop(0, ITERS, one_round, 0)

    core = lax.rem(gz, 2)
    group_a = [(dx, dc) for dx in range(nx) for dc in range(2) if (dx, dc) != (0, 0)]
    copies = []
    for k, (dx, dc) in enumerate(group_a):
        dz = 0 if dc == 0 else 1 - 2 * core
        copies.append(remote(MOM, RA.at[k], a_send.at[k], a_recv.at[k], (dx, 0, dz)))
    for c in copies:
        c.start()
    for c in copies:
        c.wait()
    total = MOM[...]
    for k in range(len(group_a)):
        total = total + RA[k]
    SB[...] = total
    group_b = [(dy, dz) for dy in range(ny) for dz in range(0, nz, 2) if (dy, dz) != (0, 0)]
    copies = []
    for k, (dy, dz) in enumerate(group_b):
        s = len(group_a) + k
        copies.append(remote(SB, RB.at[k], a_send.at[s], a_recv.at[s], (0, dy, dz)))
    for c in copies:
        c.start()
    for c in copies:
        c.wait()
    total = SB[...]
    for k in range(len(group_b)):
        total = total + RB[k]
    total = jnp.broadcast_to(jnp.sum(total, axis=1, keepdims=True), (8, LANES))
    nu = []
    for j in range(ITERS):
        a, b = total[2 * j : 2 * j + 1], total[2 * j + 1 : 2 * j + 2]
        nu += [a, b] if j == 0 else [2.0 * a - nu[0], 2.0 * b - nu[1]]
    cx, cr = cheb_coefficients(nu)
    for c in range(3):
        for i in range(NB):
            x = cx[0] * U[0, c, i]
            y = cr[0] * V[0, c, i]
            for j in range(1, ITERS):
                x = x + cx[j] * U[j, c, i]
            for j in range(1, ITERS + 1):
                y = y + cr[j] * V[j, c, i]
            XO[c, i] = x
            RO[c, i] = y
    stores = [
        pltpu.make_async_copy(XO, x_out, load_sem.at[3]),
        pltpu.make_async_copy(RO, res_out, load_sem.at[4]),
    ]
    for c in stores:
        c.start()
    for c in stores:
        c.wait()


def body(sizes, right_side, mass_coef, curl_coef):
    shape = right_side.shape
    nx, ny, nz = sizes
    n_a = 2 * nx - 1
    n_b = ny * nz // 2 - 1
    vm = lambda *s: pltpu.VMEM(s, F32)
    dma = lambda *s: pltpu.SemaphoreType.DMA(s)
    return pl.pallas_call(
        functools.partial(kernel, sizes),
        out_shape=(jax.ShapeDtypeStruct(shape, F32),) * 2,
        in_specs=[pl.BlockSpec(memory_space=pl.ANY)] * 3,
        out_specs=[pl.BlockSpec(memory_space=pl.ANY)] * 2,
        scratch_shapes=[
            vm(5, *shape),
            vm(*shape),
            vm(*shape),
            vm(*shape),
            vm(*shape[1:]),
            vm(5, 4, 10, 48, LANES),
            vm(4, *shape),
            vm(4, ROWS, LANES),
            vm(4, 8, LANES),
            vm(4, 8, LANES),
            vm(ROWS, LANES),
            vm(ROWS, LANES),
            vm(5, 7, 8, LANES),
            vm(4, 9, 8, LANES),
            vm(5, ROWS, LANES),
            vm(4, 4, ROWS, LANES),
            vm(4, 2, 8, LANES),
            vm(8, LANES),
            vm(n_a, 8, LANES),
            vm(8, LANES),
            vm(n_b, 8, LANES),
            vm(*shape),
            vm(*shape),
            dma(5),
            dma(5),
            dma(5),
            dma(4, 12),
            dma(4, 12),
            dma(n_a + n_b),
            dma(n_a + n_b),
        ],
        compiler_params=pltpu.CompilerParams(collective_id=0, has_side_effects=True),
    )(right_side, mass_coef, curl_coef)


def solution(mesh):
    sizes = (mesh.shape["gx"], mesh.shape["gy"], mesh.shape["gz"])
    spec = P(None, "gx", "gy", "gz")
    return jax.shard_map(
        functools.partial(body, sizes),
        mesh=mesh,
        in_specs=(spec,) * 3,
        out_specs=(spec,) * 2,
        check_vma=False,
    )
```

profile of v0, /device:TPU:1, one launch (start us, length us, event | category | flops | bytes accessed | tf_op | source)
XLA Modules:
  0.0 49.6 jit_solution(10183808007757062145)
XLA Ops:
  0.6 46.4 %shard_map.50 = (f32[3,8,32,128]{3,2,1,0:T(8,128)}, f32[3,8,32,128]{3,2,1,0:T(8,128)}) custom-call(f32[3,8,32,128]{3,2,1,0:T(8,128)} %r_hbm.1, f32[3,8,32,128]{3,2,1,0:T(8,128)} %m_hbm.1, f32[3,8,32,128]{3,2,1,0:T(8,128)} %k_hbm.1), custom_call_target="tpu_custom_call" | custom-call | tf_op jit(solution)/shard_map/pallas_call | solution.py:423
  47.0 0.0 copy-start
  47.0 1.8 %copy.7 = f32[3,8,32,128]{3,2,1,0:T(8,128)} copy(f32[3,8,32,128]{3,2,1,0:T(8,128)} %get-tuple-element.4) | data formatting | bytes 786432
  48.9 0.0 copy-done
  48.9 0.7 %copy.8 = f32[3,8,32,128]{3,2,1,0:T(8,128)} copy(f32[3,8,32,128]{3,2,1,0:T(8,128)S(1)} %copy-done) | data formatting | bytes 786432
Async XLA Ops:
  47.0 1.8 %copy-start = (f32[3,8,32,128]{3,2,1,0:T(8,128)S(1)}, f32[3,8,32,128]{3,2,1,0:T(8,128)}, u32[]{:S(2)}) copy-start(f32[3,8,32,128]{3,2,1,0:T(8,128)} %get-tuple-element.5) | copy-start | bytes 1179652
where the time goes:
time: 49.8 us; the launch traced here: 49.6 us
  Pallas kernels  46.4 us (93%)
  local copies, waits for them, and re-layouts  2.57 us (5%)
  between operations  0.65 us (1%)
    pallas_call x1, Pallas kernels, body(): pl.pallas_call(functools.partial(kernel, sizes), out_shape=(jax.ShapeDtyp...  46.4 us
    unnamed x4, local copies, waits for them, and re-layouts  2.57 us

commit v1 on v0

v1 whole, which is shorter than its diff:
```python
import functools
import jax
import jax.numpy as jnp
from jax import lax
from jax.experimental import pallas as pl
from jax.experimental.pallas import tpu as pltpu
from jax.sharding import PartitionSpec as P

ITERS = 4
THETA = 1.25
SIGMA = 1.25
MESH = pl.DeviceIdType.MESH
F32 = jnp.float32
NB = 8
ROWS = 32
LANES = 128
BASE = 8

ROUND = (
    (1, -1, 0),
    (-1, 1, 0),
    (1, 0, -1),
    (-1, 0, 1),
    (1, 0, 0),
    (-1, 0, 0),
    (0, 1, -1),
    (0, -1, 1),
    (0, 1, 0),
    (0, -1, 0),
    (0, 0, 1),
    (0, 0, -1),
)
EARLY = range(0, 6)
LATE = range(6, 12)
FACES = ((1, 0, 0), (-1, 0, 0), (0, 1, 0), (0, -1, 0), (0, 0, 1), (0, 0, -1))
ORDER = (7, 0, 1, 2, 3, 4, 5, 6)


def lane_id(rows=ROWS):
    return lax.broadcasted_iota(jnp.int32, (rows, LANES), 1)


def row_id(rows=ROWS):
    return lax.broadcasted_iota(jnp.int32, (rows, LANES), 0)


def roll(v, amount, axis):
    amount = amount % v.shape[axis]
    return v if amount == 0 else pltpu.roll(v, amount, axis)


def place(field, plane):
    return 16 * field + 2 * plane


def packed(acc, v, field, plane):
    at = place(field, plane)
    return jnp.where((lane_id() >> 1) == at // 2, roll(v, at - 127, 1), acc)


def below_y(v, row):
    return jnp.where(row_id() == 0, row, roll(v, 1, 0))


def below_z(v, slab, at):
    return jnp.where(lane_id() == 0, roll(slab, -at, 1), roll(v, 1, 1))


def above_z(v, slab, at):
    return jnp.where(lane_id() == 127, roll(slab, 127 - at, 1), roll(v, -1, 1))


def to_lanes(v, lane):
    out = jnp.zeros((8, LANES), F32)
    for b in range(4):
        out = jnp.where(lane_id(8) == b, roll(v[8 * b : 8 * b + 8], b - lane, 1), out)
    return out


def from_lanes(v, lane):
    return jnp.concatenate([roll(v, lane - b, 1) for b in range(4)], axis=0)


def fold(v):
    return v[0:8] + v[8:16] + v[16:24] + v[24:32]


def cheb_coefficients(nu):
    zero = jnp.zeros_like(nu[0])

    def gram(i, j):
        return 0.5 * (nu[i + j] + nu[abs(i - j)])

    def applied(c):
        out = [zero] * (len(c) + 1)
        for i, a in enumerate(c):
            if i == 0:
                out[1] = out[1] + a
            else:
                out[i + 1] = out[i + 1] + 0.5 * a
                out[i - 1] = out[i - 1] + 0.5 * a
        out = [SIGMA * a for a in out]
        for i, a in enumerate(c):
            out[i] = out[i] + THETA * a
        return out

    def dot(c, d):
        total = zero
        for i, a in enumerate(c):
            for j, b in enumerate(d):
                total = total + a * b * gram(i, j)
        return total

    res = [zero + 1.0]
    direction = None
    iterate = [zero] * ITERS
    gamma_old = alpha_old = None
    for iteration in range(ITERS):
        gamma = dot(res, res)
        delta = dot(applied(res), res)
        if iteration == 0:
            alpha = gamma / delta
            direction = list(res)
        else:
            beta = gamma / gamma_old
            alpha = gamma / (delta - beta * gamma / alpha_old)
            direction = [
                a + (beta * direction[i] if i < len(direction) else zero) for i, a in enumerate(res)
            ]
        for i, a in enumerate(direction):
            iterate[i] = iterate[i] + alpha * a
        image = applied(direction)
        res = [(res[i] if i < len(res) else zero) - alpha * a for i, a in enumerate(image)]
        gamma_old, alpha_old = gamma, alpha
    return iterate, res


def kernel(
    sizes,
    r_hbm,
    m_hbm,
    k_hbm,
    x_out,
    res_out,
    V,
    M,
    K,
    ID,
    IDN,
    F,
    U,
    G,
    CX,
    CYS,
    CY,
    CZS,
    CZ,
    YS,
    YR,
    ZS,
    ZR,
    DS,
    DR,
    LOW,
    MOM,
    RA,
    SB,
    RB,
    load_sem,
    c_send,
    c_recv,
    n_send,
    n_recv,
    a_send,
    a_recv,
):
    nx, ny, nz = sizes
    gx, gy, gz = lax.axis_index("gx"), lax.axis_index("gy"), lax.axis_index("gz")

    def device(dx, dy, dz):
        return {
            "gx": lax.rem(gx + dx + nx, nx),
            "gy": lax.rem(gy + dy + ny, ny),
            "gz": lax.rem(gz + dz + nz, nz),
        }

    def remote(src, dst, send, recv, offset):
        return pltpu.make_async_remote_copy(
            src_ref=src,
            dst_ref=dst,
            send_sem=send,
            recv_sem=recv,
            device_id=device(*offset),
            device_id_type=MESH,
        )

    loads = [
        pltpu.make_async_copy(k_hbm, K, load_sem.at[0]),
        pltpu.make_async_copy(m_hbm, M, load_sem.at[1]),
        pltpu.make_async_copy(r_hbm, V.at[0], load_sem.at[2]),
    ]
    for c in loads:
        c.start()
    barrier = pltpu.get_barrier_semaphore()
    for o in FACES:
        pl.semaphore_signal(barrier, inc=1, device_id=device(*o), device_id_type=MESH)
    for c in loads:
        c.wait()
    y_fields = (K.at[0], K.at[2], M.at[1], V.at[0, 1])
    z_fields = (K.at[0], K.at[1], M.at[2], V.at[0, 2])
    for f, ref in enumerate(y_fields):
        for i in range(NB):
            CYS[f, i : i + 1, :] = ref[i, 31:32, :]
    slab = jnp.zeros((ROWS, LANES), F32)
    for f, ref in enumerate(z_fields):
        for i in range(NB):
            slab = packed(slab, ref[i], f, i)
    CZS[...] = slab
    pl.semaphore_wait(barrier, len(FACES))
    coef = [
        remote(K.at[1:3, NB - 1], CX.at[0:2], c_send.at[0], c_recv.at[0], (1, 0, 0)),
        remote(M.at[0, NB - 1], CX.at[2], c_send.at[1], c_recv.at[1], (1, 0, 0)),
        remote(V.at[0, 0, NB - 1], CX.at[3], c_send.at[2], c_recv.at[2], (1, 0, 0)),
        remote(CYS, CY, c_send.at[3], c_recv.at[3], (0, 1, 0)),
        remote(CZS, CZ, c_send.at[4], c_recv.at[4], (0, 0, 1)),
    ]
    for c in coef:
        c.start()
    for c in coef:
        c.wait_recv()

    def messages(j, which):
        pairs = (
            (DS.at[j, 0], DR.at[j, 0]),
            (DS.at[j, 1], DR.at[j, 1]),
            (DS.at[j, 2], DR.at[j, 2]),
            (DS.at[j, 3], DR.at[j, 3]),
            (F.at[j, 0:4, NB, BASE : BASE + ROWS], F.at[j, 0:4, 0, BASE : BASE + ROWS]),
            (F.at[j, 1:4, 1, BASE : BASE + ROWS], F.at[j, 1:4, NB + 1, BASE : BASE + ROWS]),
            (YS.at[j, 1], DR.at[j, 4]),
            (ZS.at[j, 0:8], DR.at[j, 5]),
            (YS.at[j, 0:4], YR.at[j, 0:4]),
            (YS.at[j, 4:7], YR.at[j, 4:7]),
            (ZS.at[j], ZR.at[j, 0]),
            (ZS.at[j], ZR.at[j, 1]),
        )
        return [
            remote(*pairs[k], n_send.at[j, k], n_recv.at[j, k], ROUND[k]) for k in which
        ]

    def send(j, which):
        for c in messages(j, which):
            c.start()

    def receive(j):
        for c in messages(j, (0, 1, 2, 3, 6, 7, 8, 9, 10, 11, 4, 5)):
            c.wait_recv()

    def finish(j, i, slab, values):
        for f, v in enumerate(values):
            F[j, f, 1 + i, BASE : BASE + ROWS, :] = v
            YS[j, f, i : i + 1, :] = v[31:32]
            if f != 1:
                YS[j, (4, 0, 5, 6)[f], i : i + 1, :] = v[0:1]
            slab = packed(slab, v, f, i)
        if i == NB - 1:
            DS[j, 0] = jnp.broadcast_to(values[0][0:1], (8, LANES))
            DS[j, 2] = to_lanes(values[0], 0)
        if i == 0:
            DS[j, 1] = jnp.broadcast_to(values[1][31:32], (8, LANES))
            DS[j, 3] = to_lanes(values[2], 127)
        return slab

    slab = jnp.zeros((ROWS, LANES), F32)
    cz = CZ[...]
    for i in ORDER:
        k0, k1, k2 = K[0, i], K[1, i], K[2, i]
        m0, m1, m2 = M[0, i], M[1, i], M[2, i]
        r0, r1, r2 = V[0, 0, i], V[0, 1, i], V[0, 2, i]
        if i == 0:
            k1_lo, k2_lo, m0_lo, r0_lo = CX[0], CX[1], CX[2], CX[3]
        else:
            k1_lo, k2_lo, m0_lo, r0_lo = K[1, i - 1], K[2, i - 1], M[0, i - 1], V[0, 0, i - 1]
        k0y = below_y(k0, CY[0, i : i + 1, :])
        k2y = below_y(k2, CY[1, i : i + 1, :])
        m1y = below_y(m1, CY[2, i : i + 1, :])
        r1y = below_y(r1, CY[3, i : i + 1, :])
        k0z = below_z(k0, cz, place(0, i))
        k1z = below_z(k1, cz, place(1, i))
        m2z = below_z(m2, cz, place(2, i))
        r2z = below_z(r2, cz, place(3, i))
        id0 = 1.0 / (m0 + k1 + k1z + k2 + k2y)
        id1 = 1.0 / (m1 + k2 + k2_lo + k0 + k0z)
        id2 = 1.0 / (m2 + k0 + k0y + k1 + k1_lo)
        idn = 1.0 / (m0 + m0_lo + m1 + m1y + m2 + m2z)
        phi = idn * ((r0_lo - r0) + (r1y - r1) + (r2z - r2))
        ID[0, i], ID[1, i], ID[2, i], IDN[i] = id0, id1, id2, idn
        slab = finish(0, i, slab, (r0 * id0, r1 * id1, r2 * id2, phi))
        if i == 0:
            send(0, EARLY)
    ZS[0] = slab
    send(0, LATE)

    def field(j, f, i):
        return F[j, f, 1 + i, BASE : BASE + ROWS, :]

    def above_y(j, f, i):
        return F[j, f, 1 + i, BASE + 1 : BASE + 1 + ROWS, :]

    def edges(j):
        for f, at in ((0, 4), (2, 5), (3, 6)):
            for i in range(NB):
                F[j, f, 1 + i, BASE + ROWS : BASE + ROWS + 1, :] = YR[j, at, i : i + 1, :]
        F[j, 0, 0, BASE + ROWS : BASE + ROWS + 1, :] = DR[j, 0, 0:1, :]
        sub, lane8 = row_id(8), lane_id(8)
        s0, s1, s2, ph = YR[j, 0], YR[j, 1], YR[j, 2], YR[j, 3]
        own0, own2, own_ph = YS[j, 4], YS[j, 5], YS[j, 6]
        s1x = jnp.where(sub == 7, DR[j, 1], roll(s1, -1, 0))
        s1z = jnp.where(lane8 == 127, roll(DR[j, 4], -1, 1), roll(s1, -1, 1))
        LOW[0] = CY[0] * ((own2 - s2) - (s1z - s1))
        LOW[1] = CY[1] * ((s1x - s1) - (own0 - s0))
        LOW[2] = CY[2] * (s1 + (own_ph - ph))
        lane, row = lane_id(), row_id()
        low = jnp.where((lane & 1) == 1, ZS[j], ZR[j, 0])
        z0, z1 = low, roll(low, -16, 1)
        z2, zp = roll(low, -32, 1), roll(low, -48, 1)
        z2y = jnp.where(row == 31, roll(DR[j, 5], -32, 1)[0:1], roll(z2, -1, 0))
        z2x = jnp.where(lane == 14, from_lanes(DR[j, 3], 14), roll(z2, -2, 1))
        gz0 = cz * ((z2y - z2) - (roll(z1, -1, 1) - z1))
        gz1 = roll(cz, -16, 1) * ((roll(z0, -1, 1) - z0) - (z2x - z2))
        mz2 = roll(cz, -32, 1) * (z2 + (roll(zp, -1, 1) - zp))
        return gz0, gz1, mz2, ZR[j, 1]

    def fluxes_low(j):
        e0, e1, e2, ph = (field(j, f, -1) for f in range(4))
        n1, n2, nph = (field(j, f, 0) for f in (1, 2, 3))
        e0z = jnp.where(lane_id() == 127, from_lanes(DR[j, 2], 127), roll(e0, -1, 1))
        g1 = CX[0] * ((e0z - e0) - (n2 - e2))
        g2 = CX[1] * ((n1 - e1) - (above_y(j, 0, -1) - e0))
        return g1, g2, CX[2] * (e0 + (nph - ph))

    def fluxes_before(j, i, high):
        e0, e1, e2, ph = (field(j, f, i) for f in range(4))
        n1, n2, nph = (field(j, f, i + 1) for f in (1, 2, 3))
        e0z = above_z(e0, high, place(0, i) + 1)
        g1 = K[1, i] * ((e0z - e0) - (n2 - e2))
        g2 = K[2, i] * ((n1 - e1) - (above_y(j, 0, i) - e0))
        return g1, g2, M[0, i] * (e0 + (nph - ph))

    def fluxes(j, i, high):
        e0, e1, e2, ph = (field(j, f, i) for f in range(4))
        n1, n2, nph = (field(j, f, i + 1) for f in (1, 2, 3))
        e0z = above_z(e0, high, place(0, i) + 1)
        e1z = above_z(e1, high, place(1, i) + 1)
        phz = above_z(ph, high, place(3, i) + 1)
        c0 = (above_y(j, 2, i) - e2) - (e1z - e1)
        c1 = (e0z - e0) - (n2 - e2)
        c2 = (n1 - e1) - (above_y(j, 0, i) - e0)
        u0 = e0 + (nph - ph)
        u1 = e1 + (above_y(j, 3, i) - ph)
        u2 = e2 + (phz - ph)
        return (c0, c1, c2), (u0, u1, u2)

    def operator(i, g, f, lo, slabs):
        gz0, gz1, mz2, _ = slabs
        g0, g1, g2 = g
        f0, f1, f2 = f
        g1_lo, g2_lo, f0_lo = lo
        g0y = below_y(g0, LOW[0, i : i + 1, :])
        g2y = below_y(g2, LOW[1, i : i + 1, :])
        g0z = below_z(g0, gz0, 2 * i)
        g1z = below_z(g1, gz1, 2 * i)
        w0 = (g1z - g1) - (g2y - g2) + f0
        w1 = (g2_lo - g2) - (g0z - g0) + f1
        w2 = (g0y - g0) - (g1_lo - g1) + f2
        return w0, w1, w2

    def divergence(i, f, lo, slabs):
        f1y = below_y(f[1], LOW[2, i : i + 1, :])
        f2z = below_z(f[2], slabs[2], 2 * i)
        return IDN[i] * ((lo[2] - f[0]) + (f1y - f[1]) + (f2z - f[2]))

    def one_round(j, carry):
        receive(j)
        first = j == 0
        scale = jnp.where(first, F32(1.0 / SIGMA), F32(2.0 / SIGMA))
        back = jnp.where(first, F32(0.0), F32(1.0))
        before = jnp.maximum(j - 1, 0)
        slabs = edges(j)
        high = slabs[3]
        slab = jnp.zeros((ROWS, LANES), F32)
        uv = jnp.zeros((8, LANES), F32)
        wu = jnp.zeros((8, LANES), F32)
        for i in ORDER:
            if i == 7:
                lo = fluxes_before(j, 6, high)
            if i == 0:
                lo = fluxes_low(j)
            c, u = fluxes(j, i, high)
            g = [K[n, i] * c[n] for n in range(3)]
            f = [M[n, i] * u[n] for n in range(3)]
            w = operator(i, g, f, lo, slabs)
            q = divergence(i, f, lo, slabs)
            v = [V[j, n, i] for n in range(3)]
            w = [scale * (w[n] - THETA * v[n]) - back * V[before, n, i] for n in range(3)]
            q = scale * (q - THETA * field(j, 3, i)) - back * field(before, 3, i)
            for n in range(3):
                U[j, n, i] = u[n]
                V[j + 1, n, i] = w[n]
            slab = finish(j + 1, i, slab, [w[n] * ID[n, i] for n in range(3)] + [q])
            uv = uv + fold(v[0] * u[0] + v[1] * u[1] + v[2] * u[2])
            wu = wu + fold(w[0] * u[0] + w[1] * u[1] + w[2] * u[2])
            lo = (g[1], g[2], f[0])
            if i == 0:
                send(j + 1, EARLY)
        ZS[j + 1] = slab
        send(j + 1, LATE)
        MOM[pl.ds(2 * j, 1), :] = jnp.sum(uv, axis=0, keepdims=True)
        MOM[pl.ds(2 * j + 1, 1), :] = jnp.sum(wu, axis=0, keepdims=True)
        return carry

    last = ITERS - 1
    lax.fori_loop(0, last, one_round, 0)

    receive(last)
    slabs = edges(last)
    uv = jnp.zeros((8, LANES), F32)
    au = jnp.zeros((8, LANES), F32)
    bu = jnp.zeros((8, LANES), F32)
    for i in range(NB):
        c, u = fluxes(last, i, slabs[3])
        g = [K[n, i] * c[n] for n in range(3)]
        f = [M[n, i] * u[n] for n in range(3)]
        v = [V[last, n, i] for n in range(3)]
        b = [V[last - 1, n, i] for n in range(3)]
        for n in range(3):
            U[last, n, i] = u[n]
            G[n, i], G[3 + n, i] = g[n], f[n]
        uv = uv + fold(v[0] * u[0] + v[1] * u[1] + v[2] * u[2])
        bu = bu + fold(b[0] * u[0] + b[1] * u[1] + b[2] * u[2])
        au = au + fold(
            (g[0] * c[0] + g[1] * c[1] + g[2] * c[2]) + (f[0] * u[0] + f[1] * u[1] + f[2] * u[2])
        )
    scale = 2.0 / SIGMA
    wu = scale * (au - THETA * uv) - bu
    MOM[2 * last : 2 * last + 1, :] = jnp.sum(uv, axis=0, keepdims=True)
    MOM[2 * last + 1 : 2 * last + 2, :] = jnp.sum(wu, axis=0, keepdims=True)

    def last_planes(planes):
        for i in planes:
            if i == 0:
                lo = fluxes_low(last)
            else:
                lo = (G[1, i - 1], G[2, i - 1], G[3, i - 1])
            w = operator(i, [G[n, i] for n in range(3)], [G[3 + n, i] for n in range(3)], lo, slabs)
            for n in range(3):
                V[last + 1, n, i] = scale * (w[n] - THETA * V[last, n, i]) - V[last - 1, n, i]

    core = lax.rem(gz, 2)
    group_a = [(dx, dc) for dx in range(nx) for dc in range(2) if (dx, dc) != (0, 0)]
    sums_a = []
    for k, (dx, dc) in enumerate(group_a):
        dz = 0 if dc == 0 else 1 - 2 * core
        sums_a.append(remote(MOM, RA.at[k], a_send.at[k], a_recv.at[k], (dx, 0, dz)))
    for c in sums_a:
        c.start()
    last_planes(range(0, 4))
    for c in sums_a:
        c.wait_recv()
    total = MOM[...]
    for k in range(len(group_a)):
        total = total + RA[k]
    SB[...] = total
    group_b = [(dy, dz) for dy in range(ny) for dz in range(0, nz, 2) if (dy, dz) != (0, 0)]
    sums_b = []
    for k, (dy, dz) in enumerate(group_b):
        s = len(group_a) + k
        sums_b.append(remote(SB, RB.at[k], a_send.at[s], a_recv.at[s], (0, dy, dz)))
    for c in sums_b:
        c.start()
    last_planes(range(4, 8))

    def sent(j, carry):
        for c in messages(j, range(12)):
            c.wait_send()
        return carry

    lax.fori_loop(0, ITERS, sent, 0)
    for c in coef + sums_a:
        c.wait_send()
    for c in sums_b:
        c.wait_recv()
    total = SB[...]
    for k in range(len(group_b)):
        total = total + RB[k]
    total = jnp.broadcast_to(jnp.sum(total, axis=1, keepdims=True), (8, LANES))
    nu = []
    for j in range(ITERS):
        a, b = total[2 * j : 2 * j + 1], total[2 * j + 1 : 2 * j + 2]
        nu += [a, b] if j == 0 else [2.0 * a - nu[0], 2.0 * b - nu[1]]
    cx, cr = cheb_coefficients(nu)
    for c in range(3):
        for i in range(NB):
            x = cx[0] * U[0, c, i]
            y = cr[0] * V[0, c, i]
            for j in range(1, ITERS):
                x = x + cx[j] * U[j, c, i]
            for j in range(1, ITERS + 1):
                y = y + cr[j] * V[j, c, i]
            x_out[c, i] = x
            res_out[c, i] = y
    for c in sums_b:
        c.wait_send()


def body(sizes, right_side, mass_coef, curl_coef):
    shape = right_side.shape
    nx, ny, nz = sizes
    n_a = 2 * nx - 1
    n_b = ny * nz // 2 - 1
    vm = lambda *s: pltpu.VMEM(s, F32)
    dma = lambda *s: pltpu.SemaphoreType.DMA(s)
    return pl.pallas_call(
        functools.partial(kernel, sizes),
        out_shape=(pltpu.VMEM(shape, F32),) * 2,
        in_specs=[pl.BlockSpec(memory_space=pl.ANY)] * 3,
        out_specs=[pl.BlockSpec(memory_space=pltpu.VMEM)] * 2,
        scratch_shapes=[
            vm(5, *shape),
            vm(*shape),
            vm(*shape),
            vm(*shape),
            vm(*shape[1:]),
            vm(4, 4, 10, 48, LANES),
            vm(4, *shape),
            vm(6, *shape[1:]),
            vm(4, ROWS, LANES),
            vm(4, 8, LANES),
            vm(4, 8, LANES),
            vm(ROWS, LANES),
            vm(ROWS, LANES),
            vm(4, 7, 8, LANES),
            vm(4, 7, 8, LANES),
            vm(4, ROWS, LANES),
            vm(4, 2, ROWS, LANES),
            vm(4, 4, 8, LANES),
            vm(4, 6, 8, LANES),
            vm(3, 8, LANES),
            vm(8, LANES),
            vm(n_a, 8, LANES),
            vm(8, LANES),
            vm(n_b, 8, LANES),
            dma(3),
            dma(5),
            dma(5),
            dma(4, 12),
            dma(4, 12),
            dma(n_a + n_b),
            dma(n_a + n_b),
        ],
        compiler_params=pltpu.CompilerParams(collective_id=0, has_side_effects=True),
    )(right_side, mass_coef, curl_coef)


def solution(mesh):
    sizes = (mesh.shape["gx"], mesh.shape["gy"], mesh.shape["gz"])
    spec = P(None, "gx", "gy", "gz")
    return jax.shard_map(
        functools.partial(body, sizes),
        mesh=mesh,
        in_specs=(spec,) * 3,
        out_specs=(spec,) * 2,
        check_vma=False,
    )
```

time: 49.8 us -> 41.3 us (0.83)
  Pallas kernels: 46.4 us -> 39 us
  local copies, waits for them, and re-layouts: 2.57 us -> 1.49 us
    pallas_call x1, Pallas kernels: 46.4 us -> 39 us  [body(): pl.pallas_call(functools.partial(kernel, sizes), out_shape=(pltpu.VMEM(sh...]
    unnamed x4 -> x2, local copies, waits for them, and re-layouts: 2.57 us -> 1.49 us
where the time goes in v1:
time: 41.3 us; the launch traced here: 41.1 us
  Pallas kernels  39 us (94%)
  local copies, waits for them, and re-layouts  1.49 us (4%)
  between operations  0.64 us (2%)
    pallas_call x1, Pallas kernels, body(): pl.pallas_call(functools.partial(kernel, sizes), out_shape=(pltpu.VMEM(sh...  39 us
    unnamed x2, local copies, waits for them, and re-layouts  1.49 us

profile of v1, /device:TPU:1, one launch (start us, length us, event | category | flops | bytes accessed | tf_op | source)
XLA Modules:
  0.0 41.1 jit_solution(4035657970360055519)
XLA Ops:
  0.6 39.0 %shard_map.50 = (f32[3,8,32,128]{3,2,1,0:T(8,128)S(1)}, f32[3,8,32,128]{3,2,1,0:T(8,128)S(1)}) custom-call(f32[3,8,32,128]{3,2,1,0:T(8,128)} %r_hbm.1, f32[3,8,32,128]{3,2,1,0:T(8,128)} %m_hbm.1, f32[3,8,32,128]{3,2,1,0:T(8,128)} %k_hbm.1), custom_call_target="tpu_custom_call" | custom-call | tf_op jit(solution)/shard_map/pallas_call | solution.py:523
  39.6 0.7 %copy.7 = f32[3,8,32,128]{3,2,1,0:T(8,128)} copy(f32[3,8,32,128]{3,2,1,0:T(8,128)S(1)} %get-tuple-element.2) | data formatting | bytes 786432
  40.4 0.7 %copy.8 = f32[3,8,32,128]{3,2,1,0:T(8,128)} copy(f32[3,8,32,128]{3,2,1,0:T(8,128)S(1)} %get-tuple-element.3) | data formatting | bytes 786432

commit v2 on v1

v2 whole, which is shorter than its diff:
```python
import functools
import jax
import jax.numpy as jnp
from jax import lax
from jax.experimental import pallas as pl
from jax.experimental.pallas import tpu as pltpu
from jax.sharding import PartitionSpec as P

ITERS = 4
THETA = 1.25
SIGMA = 1.25
MESH = pl.DeviceIdType.MESH
F32 = jnp.float32
NB = 8
ROWS = 32
LANES = 128
BASE = 8

ROUND = (
    (1, -1, 0),
    (-1, 1, 0),
    (1, 0, -1),
    (-1, 0, 1),
    (1, 0, 0),
    (-1, 0, 0),
    (0, 1, -1),
    (0, -1, 1),
    (0, 1, 0),
    (0, -1, 0),
    (0, 0, 1),
    (0, 0, -1),
)
EARLY = range(0, 6)
LATE = range(6, 12)
FACES = ((1, 0, 0), (-1, 0, 0), (0, 1, 0), (0, -1, 0), (0, 0, 1), (0, 0, -1))
ORDER = (7, 0, 1, 2, 3, 4, 5, 6)


def lane_id(rows=ROWS):
    return lax.broadcasted_iota(jnp.int32, (rows, LANES), 1)


def row_id(rows=ROWS):
    return lax.broadcasted_iota(jnp.int32, (rows, LANES), 0)


def roll(v, amount, axis):
    amount = amount % v.shape[axis]
    return v if amount == 0 else pltpu.roll(v, amount, axis)


def place(field, plane):
    return 16 * field + 2 * plane


def packed(acc, v, field, plane):
    at = place(field, plane)
    return jnp.where((lane_id() >> 1) == at // 2, roll(v, at - 127, 1), acc)


def below_y(v, row):
    return jnp.where(row_id() == 0, row, roll(v, 1, 0))


def below_z(v, halo):
    return jnp.where(lane_id() == 0, halo, roll(v, 1, 1))


def above_z(v, halo):
    return jnp.where(lane_id() == 127, halo, roll(v, -1, 1))


def lanes_of(parts):
    sums = jnp.sum(parts, axis=1, keepdims=True)
    return jnp.sum(jnp.where(lane_id(8) == row_id(8), sums, 0.0), axis=0, keepdims=True)


def to_lanes(v, lane):
    out = jnp.zeros((8, LANES), F32)
    for b in range(4):
        out = jnp.where(lane_id(8) == b, roll(v[8 * b : 8 * b + 8], b - lane, 1), out)
    return out


def from_lanes(v, lane):
    return jnp.concatenate([roll(v, lane - b, 1) for b in range(4)], axis=0)


def fold(v):
    return v[0:8] + v[8:16] + v[16:24] + v[24:32]


def cheb_coefficients(nu):
    zero = jnp.zeros_like(nu[0])
    top = 2 * ITERS - 1

    def gram(i, j):
        if i + j == top:
            return 0.5 * nu[abs(i - j)]
        return 0.5 * (nu[i + j] + nu[abs(i - j)])

    def applied(c):
        out = [zero] * (len(c) + 1)
        for i, a in enumerate(c):
            if i == 0:
                out[1] = out[1] + a
            else:
                out[i + 1] = out[i + 1] + 0.5 * a
                out[i - 1] = out[i - 1] + 0.5 * a
        out = [SIGMA * a for a in out]
        for i, a in enumerate(c):
            out[i] = out[i] + THETA * a
        return out

    def dot(c, d):
        total = zero
        for i, a in enumerate(c):
            for j, b in enumerate(d):
                total = total + a * b * gram(i, j)
        return total

    res = [zero + 1.0]
    direction = None
    iterate = [zero] * ITERS
    gamma_old = alpha_old = None
    for iteration in range(ITERS):
        gamma = dot(res, res)
        image = applied(res)
        delta = dot(image, res)
        if iteration == 0:
            alpha = gamma / delta
            direction = list(res)
        else:
            beta = gamma / gamma_old
            slack = delta - beta * gamma / alpha_old
            direction = [
                a + (beta * direction[i] if i < len(direction) else zero) for i, a in enumerate(res)
            ]
            if iteration == ITERS - 1:
                return iterate, direction, res, applied(direction), gamma, slack, 0.5 * image[-1] * res[-1]
            alpha = gamma / slack
        for i, a in enumerate(direction):
            iterate[i] = iterate[i] + alpha * a
        step = applied(direction)
        res = [(res[i] if i < len(res) else zero) - alpha * a for i, a in enumerate(step)]
        gamma_old, alpha_old = gamma, alpha


def kernel(
    sizes,
    r_hbm,
    m_hbm,
    k_hbm,
    x_out,
    p_out,
    r_out,
    a_out,
    alpha_out,
    V,
    M,
    K,
    ID,
    IDN,
    F,
    U,
    G,
    XS,
    CX,
    CYS,
    CY,
    CZS,
    CZ,
    CZR,
    YS,
    YR,
    ZS,
    ZR,
    DS,
    DR,
    LOW,
    DN,
    MOM,
    SUM,
    RA,
    RA2,
    RB,
    RB2,
    load_sem,
    c_send,
    c_recv,
    n_send,
    n_recv,
    a_send,
    a_recv,
):
    nx, ny, nz = sizes
    gx, gy, gz = lax.axis_index("gx"), lax.axis_index("gy"), lax.axis_index("gz")

    def device(dx, dy, dz):
        return {
            "gx": lax.rem(gx + dx + nx, nx),
            "gy": lax.rem(gy + dy + ny, ny),
            "gz": lax.rem(gz + dz + nz, nz),
        }

    def remote(src, dst, send, recv, offset):
        return pltpu.make_async_remote_copy(
            src_ref=src,
            dst_ref=dst,
            send_sem=send,
            recv_sem=recv,
            device_id=device(*offset),
            device_id_type=MESH,
        )

    loads = [
        pltpu.make_async_copy(k_hbm, K, load_sem.at[0]),
        pltpu.make_async_copy(m_hbm, M, load_sem.at[1]),
        pltpu.make_async_copy(r_hbm, V.at[0], load_sem.at[2]),
    ]
    first = [
        pltpu.make_async_copy(k_hbm.at[1:3, NB - 1], XS.at[0:2], load_sem.at[3]),
        pltpu.make_async_copy(m_hbm.at[0, NB - 1], XS.at[2], load_sem.at[4]),
        pltpu.make_async_copy(r_hbm.at[0, NB - 1], XS.at[3], load_sem.at[5]),
    ]
    for c in first:
        c.start()
    for c in loads:
        c.start()
    barrier = pltpu.get_barrier_semaphore()
    for o in FACES:
        pl.semaphore_signal(barrier, inc=1, device_id=device(*o), device_id_type=MESH)
    coef = [
        remote(XS, CX, c_send.at[0], c_recv.at[0], (1, 0, 0)),
        remote(CYS, CY, c_send.at[1], c_recv.at[1], (0, 1, 0)),
        remote(CZS, CZ, c_send.at[2], c_recv.at[2], (0, 0, 1)),
    ]
    for c in first:
        c.wait()
    pl.semaphore_wait(barrier, len(FACES))
    coef[0].start()
    for c in loads:
        c.wait()
    y_fields = (K.at[0], K.at[2], M.at[1], V.at[0, 1])
    z_fields = (K.at[0], K.at[1], M.at[2], V.at[0, 2])
    for f, ref in enumerate(y_fields):
        for i in range(NB):
            CYS[f, i : i + 1, :] = ref[i, 31:32, :]
    coef[1].start()
    slab = jnp.zeros((ROWS, LANES), F32)
    for f, ref in enumerate(z_fields):
        for i in range(NB):
            slab = packed(slab, ref[i], f, i)
    CZS[...] = slab
    coef[2].start()
    for c in coef:
        c.wait_recv()

    def messages(j, which):
        pairs = (
            (DS.at[j, 0], DR.at[j, 0]),
            (DS.at[j, 1], DR.at[j, 1]),
            (DS.at[j, 2], DR.at[j, 2]),
            (DS.at[j, 3], DR.at[j, 3]),
            (F.at[j, 0:4, NB, BASE : BASE + ROWS], F.at[j, 0:4, 0, BASE : BASE + ROWS]),
            (F.at[j, 1:4, 1, BASE : BASE + ROWS], F.at[j, 1:4, NB + 1, BASE : BASE + ROWS]),
            (YS.at[j, 1], DR.at[j, 4]),
            (ZS.at[j, 0:8], DR.at[j, 5]),
            (YS.at[j, 0:4], YR.at[j, 0:4]),
            (YS.at[j, 4:7], YR.at[j, 4:7]),
            (ZS.at[j], ZR.at[j, 0]),
            (ZS.at[j], ZR.at[j, 1]),
        )
        return [
            remote(*pairs[k], n_send.at[j, k], n_recv.at[j, k], ROUND[k]) for k in which
        ]

    def send(j, which):
        for c in messages(j, which):
            c.start()

    def receive(j, which):
        for c in messages(j, which):
            c.wait_recv()

    def finish(j, i, slab, values):
        for f, v in enumerate(values):
            F[j, f, 1 + i, BASE : BASE + ROWS, :] = v
            YS[j, f, i : i + 1, :] = v[31:32]
            if f != 1:
                YS[j, (4, 0, 5, 6)[f], i : i + 1, :] = v[0:1]
            slab = packed(slab, v, f, i)
        if i == NB - 1:
            DS[j, 0] = jnp.broadcast_to(values[0][0:1], (8, LANES))
            DS[j, 2] = to_lanes(values[0], 0)
        if i == 0:
            DS[j, 1] = jnp.broadcast_to(values[1][31:32], (8, LANES))
            DS[j, 3] = to_lanes(values[2], 127)
        return slab

    slab = jnp.zeros((ROWS, LANES), F32)
    uv = jnp.zeros((8, LANES), F32)
    cz = CZ[...]
    for f in range(3):
        CZR[f] = roll(cz, 2 - 16 * f, 1)
    for i in ORDER:
        k0, k1, k2 = K[0, i], K[1, i], K[2, i]
        m0, m1, m2 = M[0, i], M[1, i], M[2, i]
        r0, r1, r2 = V[0, 0, i], V[0, 1, i], V[0, 2, i]
        if i == 0:
            k1_lo, k2_lo, m0_lo, r0_lo = CX[0], CX[1], CX[2], CX[3]
        else:
            k1_lo, k2_lo, m0_lo, r0_lo = K[1, i - 1], K[2, i - 1], M[0, i - 1], V[0, 0, i - 1]
        k0y = below_y(k0, CY[0, i : i + 1, :])
        k2y = below_y(k2, CY[1, i : i + 1, :])
        m1y = below_y(m1, CY[2, i : i + 1, :])
        r1y = below_y(r1, CY[3, i : i + 1, :])
        k0z = below_z(k0, roll(cz, -place(0, i), 1))
        k1z = below_z(k1, roll(cz, -place(1, i), 1))
        m2z = below_z(m2, roll(cz, -place(2, i), 1))
        r2z = below_z(r2, roll(cz, -place(3, i), 1))
        id0 = 1.0 / (m0 + k1 + k1z + k2 + k2y)
        id1 = 1.0 / (m1 + k2 + k2_lo + k0 + k0z)
        id2 = 1.0 / (m2 + k0 + k0y + k1 + k1_lo)
        dn = m0 + m0_lo + m1 + m1y + m2 + m2z
        idn = 1.0 / dn
        phi = idn * ((r0_lo - r0) + (r1y - r1) + (r2z - r2))
        ID[0, i], ID[1, i], ID[2, i], IDN[i], DN[i] = id0, id1, id2, idn, dn
        s0, s1, s2 = r0 * id0, r1 * id1, r2 * id2
        slab = finish(0, i, slab, (s0, s1, s2, phi))
        uv = uv + fold(r0 * s0 + r1 * s1 + r2 * s2 + dn * phi * phi)
        if i == 0:
            send(0, EARLY)
    ZS[0] = slab
    send(0, LATE)
    MOM[7:8, :] = jnp.zeros((1, LANES), F32)
    MOM[0:1, :] = jnp.sum(uv, axis=0, keepdims=True)

    def field(j, f, i):
        return F[j, f, 1 + i, BASE : BASE + ROWS, :]

    def above_y(j, f, i):
        return F[j, f, 1 + i, BASE + 1 : BASE + 1 + ROWS, :]

    def rows_above(j):
        for f, at in ((0, 4), (2, 5), (3, 6)):
            for i in range(NB):
                F[j, f, 1 + i, BASE + ROWS : BASE + ROWS + 1, :] = YR[j, at, i : i + 1, :]

    def edges(j):
        F[j, 0, 0, BASE + ROWS : BASE + ROWS + 1, :] = DR[j, 0, 0:1, :]
        sub, lane8 = row_id(8), lane_id(8)
        s0, s1, s2, ph = YR[j, 0], YR[j, 1], YR[j, 2], YR[j, 3]
        own0, own2, own_ph = YS[j, 4], YS[j, 5], YS[j, 6]
        s1x = jnp.where(sub == 7, DR[j, 1], roll(s1, -1, 0))
        s1z = jnp.where(lane8 == 127, roll(DR[j, 4], -1, 1), roll(s1, -1, 1))
        LOW[0] = CY[0] * ((own2 - s2) - (s1z - s1))
        LOW[1] = CY[1] * ((s1x - s1) - (own0 - s0))
        LOW[2] = CY[2] * (s1 + (own_ph - ph))
        lane, row = lane_id(), row_id()
        low = jnp.where((lane & 1) == 1, ZS[j], ZR[j, 0])
        z0, z1, z2, zp = (roll(low, 2 - 16 * f, 1) for f in range(4))
        z2y = jnp.where(row == 31, roll(DR[j, 5], 2 - 32, 1)[0:1], roll(z2, -1, 0))
        z2x = jnp.where(lane == 16, from_lanes(DR[j, 3], 16), roll(z2, -2, 1))
        gz0 = CZR[0] * ((z2y - z2) - (roll(z1, -1, 1) - z1))
        gz1 = CZR[1] * ((roll(z0, -1, 1) - z0) - (z2x - z2))
        mz2 = CZR[2] * (z2 + (roll(zp, -1, 1) - zp))
        odd = (lane & 1) == 1
        high = ZR[j, 1]
        return (
            jnp.where(odd, high, gz1),
            jnp.where(odd, roll(high, -16, 1), gz0),
            jnp.where(odd, roll(high, -48, 1), mz2),
        )

    def halo(slabs, i):
        return [roll(t, 126 - 2 * i, 1) for t in slabs]

    def fluxes_low(j):
        e0, e1, e2, ph = (field(j, f, -1) for f in range(4))
        n1, n2, nph = (field(j, f, 0) for f in (1, 2, 3))
        e0z = jnp.where(lane_id() == 127, from_lanes(DR[j, 2], 127), roll(e0, -1, 1))
        g1 = CX[0] * ((e0z - e0) - (n2 - e2))
        g2 = CX[1] * ((n1 - e1) - (above_y(j, 0, -1) - e0))
        return g1, g2, CX[2] * (e0 + (nph - ph))

    def fluxes_before(j, i, slabs):
        e0, e1, e2, ph = (field(j, f, i) for f in range(4))
        n1, n2, nph = (field(j, f, i + 1) for f in (1, 2, 3))
        e0z = above_z(e0, roll(slabs[0], 126 - 2 * i, 1))
        g1 = K[1, i] * ((e0z - e0) - (n2 - e2))
        g2 = K[2, i] * ((n1 - e1) - (above_y(j, 0, i) - e0))
        return g1, g2, M[0, i] * (e0 + (nph - ph))

    def fluxes(j, i, ends):
        e0, e1, e2, ph = (field(j, f, i) for f in range(4))
        n1, n2, nph = (field(j, f, i + 1) for f in (1, 2, 3))
        e0z = above_z(e0, ends[0])
        e1z = above_z(e1, ends[1])
        phz = above_z(ph, ends[2])
        c0 = (above_y(j, 2, i) - e2) - (e1z - e1)
        c1 = (e0z - e0) - (n2 - e2)
        c2 = (n1 - e1) - (above_y(j, 0, i) - e0)
        u0 = e0 + (nph - ph)
        u1 = e1 + (above_y(j, 3, i) - ph)
        u2 = e2 + (phz - ph)
        return (c0, c1, c2), (u0, u1, u2)

    def operator(i, g, f, lo, ends):
        g0, g1, g2 = g
        f0, f1, f2 = f
        g1_lo, g2_lo, f0_lo = lo
        g0y = below_y(g0, LOW[0, i : i + 1, :])
        g2y = below_y(g2, LOW[1, i : i + 1, :])
        g0z = below_z(g0, ends[1])
        g1z = below_z(g1, ends[0])
        w0 = (g1z - g1) - (g2y - g2) + f0
        w1 = (g2_lo - g2) - (g0z - g0) + f1
        w2 = (g0y - g0) - (g1_lo - g1) + f2
        return w0, w1, w2

    def divergence(i, f, lo, ends):
        f1y = below_y(f[1], LOW[2, i : i + 1, :])
        f2z = below_z(f[2], ends[2])
        return IDN[i] * ((lo[2] - f[0]) + (f1y - f[1]) + (f2z - f[2]))

    def one_round(j, carry):
        receive(j, (0, 1, 2, 3, 6, 7, 8, 9, 10, 11, 4, 5))
        first = j == 0
        scale = jnp.where(first, F32(1.0 / SIGMA), F32(2.0 / SIGMA))
        back = jnp.where(first, F32(0.0), F32(1.0))
        before = jnp.maximum(j - 1, 0)
        rows_above(j)
        slabs = edges(j)
        slab = jnp.zeros((ROWS, LANES), F32)
        uv = jnp.zeros((8, LANES), F32)
        wu = jnp.zeros((8, LANES), F32)
        for i in ORDER:
            if i == 7:
                lo = fluxes_before(j, 6, slabs)
            if i == 0:
                lo = fluxes_low(j)
            ends = halo(slabs, i)
            c, u = fluxes(j, i, ends)
            g = [K[n, i] * c[n] for n in range(3)]
            f = [M[n, i] * u[n] for n in range(3)]
            w = operator(i, g, f, lo, ends)
            q = divergence(i, f, lo, ends)
            v = [V[j, n, i] for n in range(3)]
            w = [scale * (w[n] - THETA * v[n]) - back * V[before, n, i] for n in range(3)]
            q = scale * (q - THETA * field(j, 3, i)) - back * field(before, 3, i)
            for n in range(3):
                U[j, n, i] = u[n]
                V[j + 1, n, i] = w[n]
            s = [w[n] * ID[n, i] for n in range(3)]
            slab = finish(j + 1, i, slab, s + [q])
            uv = uv + fold(w[0] * s[0] + w[1] * s[1] + w[2] * s[2] + DN[i] * q * q)
            wu = wu + fold(w[0] * u[0] + w[1] * u[1] + w[2] * u[2])
            lo = (g[1], g[2], f[0])
            if i == 0:
                send(j + 1, EARLY)
        ZS[j + 1] = slab
        send(j + 1, LATE)
        MOM[pl.ds(2 * j + 1, 1), :] = jnp.sum(wu, axis=0, keepdims=True)
        MOM[pl.ds(2 * j + 2, 1), :] = jnp.sum(uv, axis=0, keepdims=True)
        return carry

    last = ITERS - 1
    lax.fori_loop(0, last, one_round, 0)

    core = lax.rem(gz, 2)
    group_a = [
        (dx, 0, 0 if dc == 0 else 1 - 2 * core)
        for dx in range(nx)
        for dc in range(2)
        if (dx, dc) != (0, 0)
    ]
    group_b = [(0, dy, dz) for dy in range(ny) for dz in range(0, nz, 2) if (dy, dz) != (0, 0)]

    def spread(n, group, base, into):
        copies = [
            remote(SUM.at[n], into.at[k], a_send.at[base + k], a_recv.at[base + k], offset)
            for k, offset in enumerate(group)
        ]
        for c in copies:
            c.start()
        return copies

    def gather(n, copies, group, base, into):
        for c in copies:
            c.wait_recv()
        return SUM[n] + jnp.sum(into[base : base + len(group)], axis=0)

    n_a, n_b = len(group_a), len(group_b)
    SUM[0] = lanes_of(MOM[...])
    copies_0 = spread(0, group_a, 0, RA)

    receive(last, (9, 11, 5))
    rows_above(last)
    high = ZR[last, 1]
    au = jnp.zeros((8, LANES), F32)
    for i in range(NB):
        ends = [roll(high, 127 - place(f, i) - 1, 1) for f in (0, 1, 3)]
        c, u = fluxes(last, i, ends)
        g = [K[n, i] * c[n] for n in range(3)]
        f = [M[n, i] * u[n] for n in range(3)]
        for n in range(3):
            U[last, n, i] = u[n]
            G[n, i], G[3 + n, i] = g[n], f[n]
        au = au + fold(
            (g[0] * c[0] + g[1] * c[1] + g[2] * c[2]) + (f[0] * u[0] + f[1] * u[1] + f[2] * u[2])
        )
    au = jnp.sum(jnp.sum(au, axis=0, keepdims=True), axis=1, keepdims=True)
    SUM[1] = jnp.broadcast_to(au, (1, LANES))
    copies_1 = spread(1, group_a, n_a, RA2)
    SUM[2] = gather(0, copies_0, group_a, 0, RA)
    copies_2 = spread(2, group_b, 2 * n_a, RB)
    receive(last, (0, 1, 2, 3, 6, 7, 8, 10, 4))
    slabs = edges(last)
    scale = 2.0 / SIGMA

    def last_planes(planes):
        for i in planes:
            if i == 0:
                lo = fluxes_low(last)
            else:
                lo = (G[1, i - 1], G[2, i - 1], G[3, i - 1])
            ends = halo(slabs[0:2], i)
            w = operator(i, [G[n, i] for n in range(3)], [G[3 + n, i] for n in range(3)], lo, ends)
            for n in range(3):
                V[last + 1, n, i] = scale * (w[n] - THETA * V[last, n, i]) - V[last - 1, n, i]

    last_planes(range(0, NB))
    SUM[3] = gather(1, copies_1, group_a, 0, RA2)
    copies_3 = spread(3, group_b, 2 * n_a + n_b, RB2)
    total = gather(2, copies_2, group_b, 0, RB)
    moment = [
        jnp.broadcast_to(jnp.sum(jnp.where(lane_id(1) == m, total, 0.0), axis=1, keepdims=True), (1, LANES))
        for m in range(2 * ITERS - 1)
    ]
    nu = moment[0:2]
    for m in range(2, 2 * ITERS - 1):
        nu.append(2.0 * moment[m] - nu[m % 2])
    cx, cp, cr, ca, gamma, slack, weight = cheb_coefficients(nu)
    for c in range(3):
        for i in range(NB):
            u = [U[j, c, i] for j in range(ITERS)]
            v = [V[j, c, i] for j in range(ITERS + 1)]
            x_out[c, i] = sum(cx[j] * u[j] for j in range(1, last)) + cx[0] * u[0]
            p_out[c, i] = sum(cp[j] * u[j] for j in range(1, ITERS)) + cp[0] * u[0]
            r_out[c, i] = sum(cr[j] * v[j] for j in range(1, ITERS)) + cr[0] * v[0]
            a_out[c, i] = sum(ca[j] * v[j] for j in range(1, ITERS + 1)) + ca[0] * v[0]

    def sent(j, carry):
        for c in messages(j, range(12)):
            c.wait_send()
        return carry

    lax.fori_loop(0, ITERS, sent, 0)
    for c in coef + copies_0 + copies_1 + copies_2 + copies_3:
        c.wait_send()
    au = gather(3, copies_3, group_b, 0, RB2)
    top = scale * (au - THETA * moment[2 * last]) - moment[2 * last - 1]
    alpha_out[...] = gamma / (slack + weight * (2.0 * top - nu[1]))


def body(sizes, right_side, mass_coef, curl_coef):
    shape = right_side.shape
    nx, ny, nz = sizes
    n_a = 2 * nx - 1
    n_b = ny * nz // 2 - 1
    vm = lambda *s: pltpu.VMEM(s, F32)
    dma = lambda *s: pltpu.SemaphoreType.DMA(s)
    x, p, r, a, alpha = pl.pallas_call(
        functools.partial(kernel, sizes),
        out_shape=(pltpu.VMEM(shape, F32),) * 4 + (pltpu.VMEM((1, LANES), F32),),
        in_specs=[pl.BlockSpec(memory_space=pl.ANY)] * 3,
        out_specs=[pl.BlockSpec(memory_space=pltpu.VMEM)] * 5,
        scratch_shapes=[
            vm(5, *shape),
            vm(*shape),
            vm(*shape),
            vm(*shape),
            vm(*shape[1:]),
            vm(4, 4, 10, 48, LANES),
            vm(4, *shape),
            vm(6, *shape[1:]),
            vm(4, ROWS, LANES),
            vm(4, ROWS, LANES),
            vm(4, 8, LANES),
            vm(4, 8, LANES),
            vm(ROWS, LANES),
            vm(ROWS, LANES),
            vm(3, ROWS, LANES),
            vm(4, 7, 8, LANES),
            vm(4, 7, 8, LANES),
            vm(4, ROWS, LANES),
            vm(4, 2, ROWS, LANES),
            vm(4, 4, 8, LANES),
            vm(4, 6, 8, LANES),
            vm(3, 8, LANES),
            vm(*shape[1:]),
            vm(8, LANES),
            vm(4, 1, LANES),
            vm(n_a, 1, LANES),
            vm(n_a, 1, LANES),
            vm(n_b, 1, LANES),
            vm(n_b, 1, LANES),
            dma(6),
            dma(3),
            dma(3),
            dma(4, 12),
            dma(4, 12),
            dma(2 * (n_a + n_b)),
            dma(2 * (n_a + n_b)),
        ],
        compiler_params=pltpu.CompilerParams(collective_id=0, has_side_effects=True),
    )(right_side, mass_coef, curl_coef)
    step = jnp.broadcast_to(alpha[0], shape)
    return x + step * p, r - step * a


def solution(mesh):
    sizes = (mesh.shape["gx"], mesh.shape["gy"], mesh.shape["gz"])
    spec = P(None, "gx", "gy", "gz")
    return jax.shard_map(
        functools.partial(body, sizes),
        mesh=mesh,
        in_specs=(spec,) * 3,
        out_specs=(spec,) * 2,
        check_vma=False,
    )
```

time: 41.3 us -> 40.3 us (0.976)
  local copies, waits for them, and re-layouts: 1.49 us -> 0 us
  other arithmetic: 0 us -> 1.04 us
  Pallas kernels: 39 us -> 38.4 us
    unnamed x2 -> x0, local copies, waits for them, and re-layouts: 1.49 us -> none
    sub x0 -> x1, other arithmetic: none -> 1.04 us  [body(): return (x + step * p, r - step * a)]
    pallas_call x1, Pallas kernels: 39 us -> 38.4 us  [body(): pl.pallas_call(functools.partial(kernel, sizes), out_shape=(pltpu.VMEM(sh...]
where the time goes in v2:
time: 40.3 us; the launch traced here: 40 us
  Pallas kernels  38.4 us (95%)
  other arithmetic  1.04 us (3%)
  between operations  0.64 us (2%)
    pallas_call x1, Pallas kernels, body(): pl.pallas_call(functools.partial(kernel, sizes), out_shape=(pltpu.VMEM(sh...  38.4 us
    sub x1, other arithmetic, body(): return (x + step * p, r - step * a)  1.04 us

profile of v2, /device:TPU:1, one launch (start us, length us, event | category | flops | bytes accessed | tf_op | source)
XLA Modules:
  0.0 40.0 jit_solution(1330259282990754347)
XLA Ops:
  0.6 38.4 %shard_map.50 = (f32[3,8,32,128]{3,2,1,0:T(8,128)S(1)}, f32[3,8,32,128]{3,2,1,0:T(8,128)S(1)}, f32[3,8,32,128]{3,2,1,0:T(8,128)S(1)}, f32[3,8,32,128]{3,2,1,0:T(8,128)S(1)}, f32[1,128]{1,0:T(1,128)S(1)}) custom-call(f32[3,8,32,128]{3,2,1,0:T(8,128)} %r_hbm.1, f32[3,8,32,128]{3,2,1,0:T(8,128)} %m_hbm.1, f32[3,8,32,128]{3,2,1,0:T(8,128)} %k_hbm.1), custom_call_target="tpu_custom_call" | custom-call | tf_op jit(solution)/shard_map/pallas_call | solution.py:574
  39.0 1.0 %multiply_subtract_fusion = (f32[3,8,32,128]{3,2,1,0:T(8,128)}, f32[3,8,32,128]{3,2,1,0:T(8,128)}) fusion(f32[3,8,32,128]{3,2,1,0:T(8,128)S(1)} %get-tuple-element.10, f32[3,8,32,128]{3,2,1,0:T(8,128)S(1)} %get-tuple-element.11, f32[128]{0:T(128)S(1)} %bitcast.1, f32[3,8,32,128]{3,2,1,0:T(8,128)S(1)} %get-tuple-element.7, f32[3,8,32,128]{3,2,1,0:T(8,128)S(1)} %get-tuple-element.9), kind=kLoop, calls=%fused_computation | loop fusion | flops 393216 | bytes 2359808 | tf_op jit(solution)/shard_map/sub | solution.py:620

commit v3 on v2

--- a/solution.py
+++ b/solution.py
@@ -30,8 +30,9 @@
     (0, 0, 1),
     (0, 0, -1),
 )
-EARLY = range(0, 6)
-LATE = range(6, 12)
+UP = (2, 0, 4)
+DOWN = (3, 1, 5)
+LATE = (6, 7, 8, 9, 10, 11)
 FACES = ((1, 0, 0), (-1, 0, 0), (0, 1, 0), (0, -1, 0), (0, 0, 1), (0, 0, -1))
 ORDER = (7, 0, 1, 2, 3, 4, 5, 6)
 
@@ -62,12 +63,12 @@
     return jnp.where(row_id() == 0, row, roll(v, 1, 0))
 
 
-def below_z(v, halo):
-    return jnp.where(lane_id() == 0, halo, roll(v, 1, 1))
-
-
-def above_z(v, halo):
-    return jnp.where(lane_id() == 127, halo, roll(v, -1, 1))
+def first_lane(halo, v):
+    return jnp.where(lane_id() == 0, halo, v)
+
+
+def last_lane(halo, v):
+    return jnp.where(lane_id() == 127, halo, v)
 
 
 def lanes_of(parts):
@@ -164,6 +165,8 @@
     F,
     U,
     G,
+    S,
+    T,
     XS,
     CX,
     CYS,
@@ -182,9 +185,9 @@
     MOM,
     SUM,
     RA,
-    RA2,
     RB,
-    RB2,
+    RC,
+    RD,
     load_sem,
     c_send,
     c_recv,
@@ -253,6 +256,11 @@
             slab = packed(slab, ref[i], f, i)
     CZS[...] = slab
     coef[2].start()
+    for i in range(NB):
+        S[0, i] = roll(K[0, i], 1, 1)
+        S[1, i] = roll(K[1, i], 1, 1)
+        S[2, i] = roll(M[2, i], 1, 1)
+        S[3, i] = roll(V[0, 2, i], 1, 1)
     for c in coef:
         c.wait_recv()
 
@@ -299,7 +307,6 @@
         return slab
 
     slab = jnp.zeros((ROWS, LANES), F32)
-    uv = jnp.zeros((8, LANES), F32)
     cz = CZ[...]
     for f in range(3):
         CZR[f] = roll(cz, 2 - 16 * f, 1)
@@ -315,10 +322,10 @@
         k2y = below_y(k2, CY[1, i : i + 1, :])
         m1y = below_y(m1, CY[2, i : i + 1, :])
         r1y = below_y(r1, CY[3, i : i + 1, :])
-        k0z = below_z(k0, roll(cz, -place(0, i), 1))
-        k1z = below_z(k1, roll(cz, -place(1, i), 1))
-        m2z = below_z(m2, roll(cz, -place(2, i), 1))
-        r2z = below_z(r2, roll(cz, -place(3, i), 1))
+        k0z = first_lane(roll(cz, -place(0, i), 1), S[0, i])
+        k1z = first_lane(roll(cz, -place(1, i), 1), S[1, i])
+        m2z = first_lane(roll(cz, -place(2, i), 1), S[2, i])
+        r2z = first_lane(roll(cz, -place(3, i), 1), S[3, i])
         id0 = 1.0 / (m0 + k1 + k1z + k2 + k2y)
         id1 = 1.0 / (m1 + k2 + k2_lo + k0 + k0z)
         id2 = 1.0 / (m2 + k0 + k0y + k1 + k1_lo)
@@ -328,13 +335,13 @@
         ID[0, i], ID[1, i], ID[2, i], IDN[i], DN[i] = id0, id1, id2, idn, dn
         s0, s1, s2 = r0 * id0, r1 * id1, r2 * id2
         slab = finish(0, i, slab, (s0, s1, s2, phi))
-        uv = uv + fold(r0 * s0 + r1 * s1 + r2 * s2 + dn * phi * phi)
+        if i == 7:
+            send(0, UP)
         if i == 0:
-            send(0, EARLY)
+            send(0, DOWN)
     ZS[0] = slab
     send(0, LATE)
     MOM[7:8, :] = jnp.zeros((1, LANES), F32)
-    MOM[0:1, :] = jnp.sum(uv, axis=0, keepdims=True)
 
     def field(j, f, i):
         return F[j, f, 1 + i, BASE : BASE + ROWS, :]
@@ -373,6 +380,28 @@
             jnp.where(odd, roll(high, -48, 1), mz2),
         )
 
+    def ahead(j):
+        first = j == 0
+        scale = jnp.where(first, F32(1.0 / SIGMA), F32(2.0 / SIGMA))
+        back = jnp.where(first, F32(0.0), F32(1.0))
+        before = jnp.maximum(j - 1, 0)
+        uv = jnp.zeros((8, LANES), F32)
+        for i in range(NB):
+            e0, e1, e2, ph = (field(j, f, i) for f in range(4))
+            v = [V[j, n, i] for n in range(3)]
+            e0z, e1z, phz = roll(e0, -1, 1), roll(e1, -1, 1), roll(ph, -1, 1)
+            S[0, i], S[1, i], S[2, i] = e0z, e1z, phz
+            c0 = (above_y(j, 2, i) - e2) - (e1z - e1)
+            S[3, i] = roll(K[0, i] * c0, 1, 1)
+            if i < NB - 1:
+                S[4, i] = roll(K[1, i] * ((e0z - e0) - (field(j, 2, i + 1) - e2)), 1, 1)
+            S[5, i] = roll(M[2, i] * (e2 + (phz - ph)), 1, 1)
+            for n in range(3):
+                T[n, i] = (scale * THETA) * v[n] + back * V[before, n, i]
+            T[3, i] = (scale * THETA) * ph + back * field(before, 3, i)
+            uv = uv + fold(v[0] * e0 + v[1] * e1 + v[2] * e2 + DN[i] * ph * ph)
+        MOM[pl.ds(2 * j, 1), :] = jnp.sum(uv, axis=0, keepdims=True)
+
     def halo(slabs, i):
         return [roll(t, 126 - 2 * i, 1) for t in slabs]
 
@@ -387,7 +416,7 @@
     def fluxes_before(j, i, slabs):
         e0, e1, e2, ph = (field(j, f, i) for f in range(4))
         n1, n2, nph = (field(j, f, i + 1) for f in (1, 2, 3))
-        e0z = above_z(e0, roll(slabs[0], 126 - 2 * i, 1))
+        e0z = last_lane(roll(slabs[0], 126 - 2 * i, 1), S[0, i])
         g1 = K[1, i] * ((e0z - e0) - (n2 - e2))
         g2 = K[2, i] * ((n1 - e1) - (above_y(j, 0, i) - e0))
         return g1, g2, M[0, i] * (e0 + (nph - ph))
@@ -395,9 +424,9 @@
     def fluxes(j, i, ends):
         e0, e1, e2, ph = (field(j, f, i) for f in range(4))
         n1, n2, nph = (field(j, f, i + 1) for f in (1, 2, 3))
-        e0z = above_z(e0, ends[0])
-        e1z = above_z(e1, ends[1])
-        phz = above_z(ph, ends[2])
+        e0z = last_lane(ends[0], S[0, i])
+        e1z = last_lane(ends[1], S[1, i])
+        phz = last_lane(ends[2], S[2, i])
         c0 = (above_y(j, 2, i) - e2) - (e1z - e1)
         c1 = (e0z - e0) - (n2 - e2)
         c2 = (n1 - e1) - (above_y(j, 0, i) - e0)
@@ -412,8 +441,9 @@
         g1_lo, g2_lo, f0_lo = lo
         g0y = below_y(g0, LOW[0, i : i + 1, :])
         g2y = below_y(g2, LOW[1, i : i + 1, :])
-        g0z = below_z(g0, ends[1])
-        g1z = below_z(g1, ends[0])
+        g0z = jnp.concatenate([S[3, i, 0:24], roll(g0[24:32], 1, 1)], axis=0)
+        g0z = first_lane(ends[1], g0z)
+        g1z = first_lane(ends[0], roll(g1, 1, 1) if i == NB - 1 else S[4, i])
         w0 = (g1z - g1) - (g2y - g2) + f0
         w1 = (g2_lo - g2) - (g0z - g0) + f1
         w2 = (g0y - g0) - (g1_lo - g1) + f2
@@ -421,20 +451,15 @@
 
     def divergence(i, f, lo, ends):
         f1y = below_y(f[1], LOW[2, i : i + 1, :])
-        f2z = below_z(f[2], ends[2])
+        f2z = first_lane(ends[2], S[5, i])
         return IDN[i] * ((lo[2] - f[0]) + (f1y - f[1]) + (f2z - f[2]))
 
     def one_round(j, carry):
         receive(j, (0, 1, 2, 3, 6, 7, 8, 9, 10, 11, 4, 5))
-        first = j == 0
-        scale = jnp.where(first, F32(1.0 / SIGMA), F32(2.0 / SIGMA))
-        back = jnp.where(first, F32(0.0), F32(1.0))
-        before = jnp.maximum(j - 1, 0)
+        scale = jnp.where(j == 0, F32(1.0 / SIGMA), F32(2.0 / SIGMA))
         rows_above(j)
         slabs = edges(j)
         slab = jnp.zeros((ROWS, LANES), F32)
-        uv = jnp.zeros((8, LANES), F32)
-        wu = jnp.zeros((8, LANES), F32)
         for i in ORDER:
             if i == 7:
                 lo = fluxes_before(j, 6, slabs)
@@ -446,26 +471,30 @@
             f = [M[n, i] * u[n] for n in range(3)]
             w = operator(i, g, f, lo, ends)
             q = divergence(i, f, lo, ends)
-            v = [V[j, n, i] for n in range(3)]
-            w = [scale * (w[n] - THETA * v[n]) - back * V[before, n, i] for n in range(3)]
-            q = scale * (q - THETA * field(j, 3, i)) - back * field(before, 3, i)
+            w = [scale * w[n] - T[n, i] for n in range(3)]
+            q = scale * q - T[3, i]
             for n in range(3):
                 U[j, n, i] = u[n]
                 V[j + 1, n, i] = w[n]
             s = [w[n] * ID[n, i] for n in range(3)]
             slab = finish(j + 1, i, slab, s + [q])
-            uv = uv + fold(w[0] * s[0] + w[1] * s[1] + w[2] * s[2] + DN[i] * q * q)
-            wu = wu + fold(w[0] * u[0] + w[1] * u[1] + w[2] * u[2])
             lo = (g[1], g[2], f[0])
+            if i == 7:
+                send(j + 1, UP)
             if i == 0:
-                send(j + 1, EARLY)
+                send(j + 1, DOWN)
         ZS[j + 1] = slab
         send(j + 1, LATE)
+        ahead(j + 1)
+        wu = jnp.zeros((8, LANES), F32)
+        for i in range(NB):
+            w = [V[j + 1, n, i] for n in range(3)]
+            wu = wu + fold(w[0] * U[j, 0, i] + w[1] * U[j, 1, i] + w[2] * U[j, 2, i])
         MOM[pl.ds(2 * j + 1, 1), :] = jnp.sum(wu, axis=0, keepdims=True)
-        MOM[pl.ds(2 * j + 2, 1), :] = jnp.sum(uv, axis=0, keepdims=True)
         return carry
 
     last = ITERS - 1
+    ahead(0)
     lax.fori_loop(0, last, one_round, 0)
 
     core = lax.rem(gz, 2)
@@ -474,6 +503,14 @@
         for dx in range(nx)
         for dc in range(2)
         if (dx, dc) != (0, 0)
+    ]
+    pair = [(0, 0, 1 - 2 * core)]
+    chips = [
+        (dx, dy, dz)
+        for dx in range(nx)
+        for dy in range(ny)
+        for dz in range(0, nz, 2)
+        if (dx, dy, dz) != (0, 0, 0)
     ]
     group_b = [(0, dy, dz) for dy in range(ny) for dz in range(0, nz, 2) if (dy, dz) != (0, 0)]
 
@@ -512,9 +549,11 @@
         )
     au = jnp.sum(jnp.sum(au, axis=0, keepdims=True), axis=1, keepdims=True)
     SUM[1] = jnp.broadcast_to(au, (1, LANES))
-    copies_1 = spread(1, group_a, n_a, RA2)
+    copies_1 = spread(1, pair, n_a + n_b, RC)
+    SUM[3] = gather(1, copies_1, pair, 0, RC)
+    copies_3 = spread(3, chips, n_a + n_b + 1, RD)
     SUM[2] = gather(0, copies_0, group_a, 0, RA)
-    copies_2 = spread(2, group_b, 2 * n_a, RB)
+    copies_2 = spread(2, group_b, n_a, RB)
     receive(last, (0, 1, 2, 3, 6, 7, 8, 10, 4))
     slabs = edges(last)
     scale = 2.0 / SIGMA
@@ -528,11 +567,9 @@
             ends = halo(slabs[0:2], i)
             w = operator(i, [G[n, i] for n in range(3)], [G[3 + n, i] for n in range(3)], lo, ends)
             for n in range(3):
-                V[last + 1, n, i] = scale * (w[n] - THETA * V[last, n, i]) - V[last - 1, n, i]
+                V[last + 1, n, i] = scale * w[n] - T[n, i]
 
     last_planes(range(0, NB))
-    SUM[3] = gather(1, copies_1, group_a, 0, RA2)
-    copies_3 = spread(3, group_b, 2 * n_a + n_b, RB2)
     total = gather(2, copies_2, group_b, 0, RB)
     moment = [
         jnp.broadcast_to(jnp.sum(jnp.where(lane_id(1) == m, total, 0.0), axis=1, keepdims=True), (1, LANES))
@@ -559,7 +596,7 @@
     lax.fori_loop(0, ITERS, sent, 0)
     for c in coef + copies_0 + copies_1 + copies_2 + copies_3:
         c.wait_send()
-    au = gather(3, copies_3, group_b, 0, RB2)
+    au = gather(3, copies_3, chips, 0, RD)
     top = scale * (au - THETA * moment[2 * last]) - moment[2 * last - 1]
     alpha_out[...] = gamma / (slack + weight * (2.0 * top - nu[1]))
 
@@ -569,6 +606,7 @@
     nx, ny, nz = sizes
     n_a = 2 * nx - 1
     n_b = ny * nz // 2 - 1
+    n_c = nx * ny * nz // 2 - 1
     vm = lambda *s: pltpu.VMEM(s, F32)
     dma = lambda *s: pltpu.SemaphoreType.DMA(s)
     x, p, r, a, alpha = pl.pallas_call(
@@ -585,6 +623,8 @@
             vm(4, 4, 10, 48, LANES),
             vm(4, *shape),
             vm(6, *shape[1:]),
+            vm(6, *shape[1:]),
+            vm(4, *shape[1:]),
             vm(4, ROWS, LANES),
             vm(4, ROWS, LANES),
             vm(4, 8, LANES),
@@ -603,16 +643,16 @@
             vm(8, LANES),
             vm(4, 1, LANES),
             vm(n_a, 1, LANES),
-            vm(n_a, 1, LANES),
             vm(n_b, 1, LANES),
-            vm(n_b, 1, LANES),
+            vm(1, 1, LANES),
+            vm(n_c, 1, LANES),
             dma(6),
             dma(3),
             dma(3),
             dma(4, 12),
             dma(4, 12),
-            dma(2 * (n_a + n_b)),
-            dma(2 * (n_a + n_b)),
+            dma(n_a + n_b + 1 + n_c),
+            dma(n_a + n_b + 1 + n_c),
         ],
         compiler_params=pltpu.CompilerParams(collective_id=0, has_side_effects=True),
     )(right_side, mass_coef, curl_coef)

time: 40.3 us -> 40.4 us (level)
  no operation moved by 1% of the time
where the time goes in v3:
time: 40.4 us; the launch traced here: 40.3 us
  Pallas kernels  38.6 us (96%)
  other arithmetic  1.04 us (3%)
  between operations  0.64 us (2%)
    pallas_call x1, Pallas kernels, body(): pl.pallas_call(functools.partial(kernel, sizes), out_shape=(pltpu.VMEM(sh...  38.6 us
    sub x1, other arithmetic, body(): return (x + step * p, r - step * a)  1.04 us

profile of v3, /device:TPU:1, one launch (start us, length us, event | category | flops | bytes accessed | tf_op | source)
XLA Modules:
  0.0 40.3 jit_solution(3314635561019722270)
XLA Ops:
  0.6 38.6 %shard_map.50 = (f32[3,8,32,128]{3,2,1,0:T(8,128)S(1)}, f32[3,8,32,128]{3,2,1,0:T(8,128)S(1)}, f32[3,8,32,128]{3,2,1,0:T(8,128)S(1)}, f32[3,8,32,128]{3,2,1,0:T(8,128)S(1)}, f32[1,128]{1,0:T(1,128)S(1)}) custom-call(f32[3,8,32,128]{3,2,1,0:T(8,128)} %r_hbm.1, f32[3,8,32,128]{3,2,1,0:T(8,128)} %m_hbm.1, f32[3,8,32,128]{3,2,1,0:T(8,128)} %k_hbm.1), custom_call_target="tpu_custom_call" | custom-call | tf_op jit(solution)/shard_map/pallas_call | solution.py:612
  39.3 1.0 %multiply_subtract_fusion = (f32[3,8,32,128]{3,2,1,0:T(8,128)}, f32[3,8,32,128]{3,2,1,0:T(8,128)}) fusion(f32[3,8,32,128]{3,2,1,0:T(8,128)S(1)} %get-tuple-element.10, f32[3,8,32,128]{3,2,1,0:T(8,128)S(1)} %get-tuple-element.11, f32[128]{0:T(128)S(1)} %bitcast.1, f32[3,8,32,128]{3,2,1,0:T(8,128)S(1)} %get-tuple-element.7, f32[3,8,32,128]{3,2,1,0:T(8,128)S(1)} %get-tuple-element.9), kind=kLoop, calls=%fused_computation | loop fusion | flops 393216 | bytes 2359808 | tf_op jit(solution)/shard_map/sub | solution.py:660

commit v4 on v3

--- a/solution.py
+++ b/solution.py
@@ -34,7 +34,7 @@
 DOWN = (3, 1, 5)
 LATE = (6, 7, 8, 9, 10, 11)
 FACES = ((1, 0, 0), (-1, 0, 0), (0, 1, 0), (0, -1, 0), (0, 0, 1), (0, 0, -1))
-ORDER = (7, 0, 1, 2, 3, 4, 5, 6)
+START = (7, 6, 5, 4, 3, 2, 1, 0)
 
 
 def lane_id(rows=ROWS):
@@ -174,6 +174,7 @@
     CZS,
     CZ,
     CZR,
+    CZ7,
     YS,
     YR,
     ZS,
@@ -261,8 +262,8 @@
         S[1, i] = roll(K[1, i], 1, 1)
         S[2, i] = roll(M[2, i], 1, 1)
         S[3, i] = roll(V[0, 2, i], 1, 1)
-    for c in coef:
-        c.wait_recv()
+    coef[1].wait_recv()
+    coef[2].wait_recv()
 
     def messages(j, which):
         pairs = (
@@ -292,25 +293,30 @@
             c.wait_recv()
 
     def finish(j, i, slab, values):
-        for f, v in enumerate(values):
+        for f, v in values.items():
             F[j, f, 1 + i, BASE : BASE + ROWS, :] = v
             YS[j, f, i : i + 1, :] = v[31:32]
             if f != 1:
                 YS[j, (4, 0, 5, 6)[f], i : i + 1, :] = v[0:1]
             slab = packed(slab, v, f, i)
-        if i == NB - 1:
-            DS[j, 0] = jnp.broadcast_to(values[0][0:1], (8, LANES))
-            DS[j, 2] = to_lanes(values[0], 0)
-        if i == 0:
-            DS[j, 1] = jnp.broadcast_to(values[1][31:32], (8, LANES))
-            DS[j, 3] = to_lanes(values[2], 127)
         return slab
+
+    def diagonals(j, s0, s1, s2):
+        if s0 is not None:
+            DS[j, 0] = jnp.broadcast_to(s0[0:1], (8, LANES))
+            DS[j, 2] = to_lanes(s0, 0)
+        if s1 is not None:
+            DS[j, 1] = jnp.broadcast_to(s1[31:32], (8, LANES))
+            DS[j, 3] = to_lanes(s2, 127)
 
     slab = jnp.zeros((ROWS, LANES), F32)
     cz = CZ[...]
     for f in range(3):
         CZR[f] = roll(cz, 2 - 16 * f, 1)
-    for i in ORDER:
+    CZ7[...] = roll(cz, -place(1, NB - 1), 1)
+    for i in START:
+        if i == 0:
+            coef[0].wait_recv()
         k0, k1, k2 = K[0, i], K[1, i], K[2, i]
         m0, m1, m2 = M[0, i], M[1, i], M[2, i]
         r0, r1, r2 = V[0, 0, i], V[0, 1, i], V[0, 2, i]
@@ -334,7 +340,8 @@
         phi = idn * ((r0_lo - r0) + (r1y - r1) + (r2z - r2))
         ID[0, i], ID[1, i], ID[2, i], IDN[i], DN[i] = id0, id1, id2, idn, dn
         s0, s1, s2 = r0 * id0, r1 * id1, r2 * id2
-        slab = finish(0, i, slab, (s0, s1, s2, phi))
+        slab = finish(0, i, slab, {0: s0, 1: s1, 2: s2, 3: phi})
+        diagonals(0, s0 if i == 7 else None, s1 if i == 0 else None, s2)
         if i == 7:
             send(0, UP)
         if i == 0:
@@ -354,12 +361,11 @@
             for i in range(NB):
                 F[j, f, 1 + i, BASE + ROWS : BASE + ROWS + 1, :] = YR[j, at, i : i + 1, :]
 
-    def edges(j):
-        F[j, 0, 0, BASE + ROWS : BASE + ROWS + 1, :] = DR[j, 0, 0:1, :]
+    def edges(j, diag):
         sub, lane8 = row_id(8), lane_id(8)
         s0, s1, s2, ph = YR[j, 0], YR[j, 1], YR[j, 2], YR[j, 3]
         own0, own2, own_ph = YS[j, 4], YS[j, 5], YS[j, 6]
-        s1x = jnp.where(sub == 7, DR[j, 1], roll(s1, -1, 0))
+        s1x = jnp.where(sub == 7, DR[j, 1] if diag else 0.0, roll(s1, -1, 0))
         s1z = jnp.where(lane8 == 127, roll(DR[j, 4], -1, 1), roll(s1, -1, 1))
         LOW[0] = CY[0] * ((own2 - s2) - (s1z - s1))
         LOW[1] = CY[1] * ((s1x - s1) - (own0 - s0))
@@ -368,7 +374,7 @@
         low = jnp.where((lane & 1) == 1, ZS[j], ZR[j, 0])
         z0, z1, z2, zp = (roll(low, 2 - 16 * f, 1) for f in range(4))
         z2y = jnp.where(row == 31, roll(DR[j, 5], 2 - 32, 1)[0:1], roll(z2, -1, 0))
-        z2x = jnp.where(lane == 16, from_lanes(DR[j, 3], 16), roll(z2, -2, 1))
+        z2x = jnp.where(lane == 16, from_lanes(DR[j, 3], 16) if diag else 0.0, roll(z2, -2, 1))
         gz0 = CZR[0] * ((z2y - z2) - (roll(z1, -1, 1) - z1))
         gz1 = CZR[1] * ((roll(z0, -1, 1) - z0) - (z2x - z2))
         mz2 = CZR[2] * (z2 + (roll(zp, -1, 1) - zp))
@@ -405,21 +411,14 @@
     def halo(slabs, i):
         return [roll(t, 126 - 2 * i, 1) for t in slabs]
 
-    def fluxes_low(j):
+    def fluxes_low(j, diag):
         e0, e1, e2, ph = (field(j, f, -1) for f in range(4))
         n1, n2, nph = (field(j, f, 0) for f in (1, 2, 3))
-        e0z = jnp.where(lane_id() == 127, from_lanes(DR[j, 2], 127), roll(e0, -1, 1))
+        e0z = last_lane(from_lanes(DR[j, 2], 127) if diag else 0.0, roll(e0, -1, 1))
+        e0y = jnp.where(row_id() == 31, DR[j, 0, 0:1, :] if diag else 0.0, roll(e0, -1, 0))
         g1 = CX[0] * ((e0z - e0) - (n2 - e2))
-        g2 = CX[1] * ((n1 - e1) - (above_y(j, 0, -1) - e0))
+        g2 = CX[1] * ((n1 - e1) - (e0y - e0))
         return g1, g2, CX[2] * (e0 + (nph - ph))
-
-    def fluxes_before(j, i, slabs):
-        e0, e1, e2, ph = (field(j, f, i) for f in range(4))
-        n1, n2, nph = (field(j, f, i + 1) for f in (1, 2, 3))
-        e0z = last_lane(roll(slabs[0], 126 - 2 * i, 1), S[0, i])
-        g1 = K[1, i] * ((e0z - e0) - (n2 - e2))
-        g2 = K[2, i] * ((n1 - e1) - (above_y(j, 0, i) - e0))
-        return g1, g2, M[0, i] * (e0 + (nph - ph))
 
     def fluxes(j, i, ends):
         e0, e1, e2, ph = (field(j, f, i) for f in range(4))
@@ -455,34 +454,58 @@
         return IDN[i] * ((lo[2] - f[0]) + (f1y - f[1]) + (f2z - f[2]))
 
     def one_round(j, carry):
-        receive(j, (0, 1, 2, 3, 6, 7, 8, 9, 10, 11, 4, 5))
+        receive(j, (6, 7, 8, 9, 10, 11))
         scale = jnp.where(j == 0, F32(1.0 / SIGMA), F32(2.0 / SIGMA))
         rows_above(j)
-        slabs = edges(j)
-        slab = jnp.zeros((ROWS, LANES), F32)
-        for i in ORDER:
-            if i == 7:
-                lo = fluxes_before(j, 6, slabs)
-            if i == 0:
-                lo = fluxes_low(j)
+        slabs = edges(j, False)
+
+        def products(i):
             ends = halo(slabs, i)
             c, u = fluxes(j, i, ends)
-            g = [K[n, i] * c[n] for n in range(3)]
-            f = [M[n, i] * u[n] for n in range(3)]
+            for n in range(3):
+                U[j, n, i] = u[n]
+            return [K[n, i] * c[n] for n in range(3)], [M[n, i] * u[n] for n in range(3)], ends
+
+        def advance(i, slab, g, f, ends, lo):
             w = operator(i, g, f, lo, ends)
             q = divergence(i, f, lo, ends)
             w = [scale * w[n] - T[n, i] for n in range(3)]
-            q = scale * q - T[3, i]
             for n in range(3):
-                U[j, n, i] = u[n]
                 V[j + 1, n, i] = w[n]
-            s = [w[n] * ID[n, i] for n in range(3)]
-            slab = finish(j + 1, i, slab, s + [q])
+            s = {n: w[n] * ID[n, i] for n in range(3)}
+            s[3] = scale * q - T[3, i]
+            if i == 0:
+                del s[1], s[2]
+            if i == NB - 1:
+                del s[0]
+            return finish(j + 1, i, slab, s)
+
+        slab = jnp.zeros((ROWS, LANES), F32)
+        g, f, ends = products(0)
+        plane_0 = (g, f, ends)
+        for i in range(1, NB):
             lo = (g[1], g[2], f[0])
-            if i == 7:
-                send(j + 1, UP)
-            if i == 0:
-                send(j + 1, DOWN)
+            if i == NB - 1:
+                receive(j, (4, 5))
+            g, f, ends = products(i)
+            slab = advance(i, slab, g, f, ends, lo)
+        slab = advance(0, slab, *plane_0, fluxes_low(j, False))
+        receive(j, (0, 1, 2, 3))
+        end = NB - 1
+        xz = jnp.where(lane_id() == 0, CZ7[...] * from_lanes(DR[j, 3], 0), 0.0)
+        xy = jnp.where(row_id() == 0, CY[1, end : end + 1, :] * DR[j, 1, 0:1, :], 0.0)
+        w0 = V[j + 1, 0, end] - scale * (xy + xz)
+        xy = jnp.where(row_id() == 31, CX[1, 31:32, :] * DR[j, 0, 0:1, :], 0.0)
+        w1 = V[j + 1, 1, 0] - scale * xy
+        xz = jnp.where(lane_id() == 127, CX[0] * from_lanes(DR[j, 2], 127), 0.0)
+        w2 = V[j + 1, 2, 0] - scale * xz
+        s0, s1, s2 = w0 * ID[0, end], w1 * ID[1, 0], w2 * ID[2, 0]
+        diagonals(j + 1, s0, s1, s2)
+        send(j + 1, (0, 1, 2, 3))
+        slab = finish(j + 1, end, slab, {0: s0})
+        slab = finish(j + 1, 0, slab, {1: s1, 2: s2})
+        send(j + 1, (4, 5))
+        V[j + 1, 0, end], V[j + 1, 1, 0], V[j + 1, 2, 0] = w0, w1, w2
         ZS[j + 1] = slab
         send(j + 1, LATE)
         ahead(j + 1)
@@ -512,6 +535,7 @@
         for dz in range(0, nz, 2)
         if (dx, dy, dz) != (0, 0, 0)
     ]
+    chips.sort(key=lambda o: -sum(min(d, n - d) for d, n in zip((o[0], o[1], o[2] // 2), (nx, ny, nz // 2))))
     group_b = [(0, dy, dz) for dy in range(ny) for dz in range(0, nz, 2) if (dy, dz) != (0, 0)]
 
     def spread(n, group, base, into):
@@ -555,13 +579,13 @@
     SUM[2] = gather(0, copies_0, group_a, 0, RA)
     copies_2 = spread(2, group_b, n_a, RB)
     receive(last, (0, 1, 2, 3, 6, 7, 8, 10, 4))
-    slabs = edges(last)
+    slabs = edges(last, True)
     scale = 2.0 / SIGMA
 
     def last_planes(planes):
         for i in planes:
             if i == 0:
-                lo = fluxes_low(last)
+                lo = fluxes_low(last, True)
             else:
                 lo = (G[1, i - 1], G[2, i - 1], G[3, i - 1])
             ends = halo(slabs[0:2], i)
@@ -632,6 +656,7 @@
             vm(ROWS, LANES),
             vm(ROWS, LANES),
             vm(3, ROWS, LANES),
+            vm(ROWS, LANES),
             vm(4, 7, 8, LANES),
             vm(4, 7, 8, LANES),
             vm(4, ROWS, LANES),

time: 40.4 us -> 39.2 us (0.970)
  Pallas kernels: 38.6 us -> 37.4 us
    pallas_call x1, Pallas kernels: 38.6 us -> 37.4 us  [body(): pl.pallas_call(functools.partial(kernel, sizes), out_shape=(pltpu.VMEM(sh...]
where the time goes in v4:
time: 39.2 us; the launch traced here: 39.1 us
  Pallas kernels  37.4 us (95%)
  other arithmetic  1.04 us (3%)
  between operations  0.64 us (2%)
    pallas_call x1, Pallas kernels, body(): pl.pallas_call(functools.partial(kernel, sizes), out_shape=(pltpu.VMEM(sh...  37.4 us
    sub x1, other arithmetic, body(): return (x + step * p, r - step * a)  1.04 us

profile of v4, /device:TPU:1, one launch (start us, length us, event | category | flops | bytes accessed | tf_op | source)
XLA Modules:
  0.0 39.1 jit_solution(757085621385409128)
XLA Ops:
  0.6 37.4 %shard_map.50 = (f32[3,8,32,128]{3,2,1,0:T(8,128)S(1)}, f32[3,8,32,128]{3,2,1,0:T(8,128)S(1)}, f32[3,8,32,128]{3,2,1,0:T(8,128)S(1)}, f32[3,8,32,128]{3,2,1,0:T(8,128)S(1)}, f32[1,128]{1,0:T(1,128)S(1)}) custom-call(f32[3,8,32,128]{3,2,1,0:T(8,128)} %r_hbm.1, f32[3,8,32,128]{3,2,1,0:T(8,128)} %m_hbm.1, f32[3,8,32,128]{3,2,1,0:T(8,128)} %k_hbm.1), custom_call_target="tpu_custom_call" | custom-call | tf_op jit(solution)/shard_map/pallas_call | solution.py:636
  38.1 1.0 %multiply_subtract_fusion = (f32[3,8,32,128]{3,2,1,0:T(8,128)}, f32[3,8,32,128]{3,2,1,0:T(8,128)}) fusion(f32[3,8,32,128]{3,2,1,0:T(8,128)S(1)} %get-tuple-element.10, f32[3,8,32,128]{3,2,1,0:T(8,128)S(1)} %get-tuple-element.11, f32[128]{0:T(128)S(1)} %bitcast.1, f32[3,8,32,128]{3,2,1,0:T(8,128)S(1)} %get-tuple-element.7, f32[3,8,32,128]{3,2,1,0:T(8,128)S(1)} %get-tuple-element.9), kind=kLoop, calls=%fused_computation | loop fusion | flops 393216 | bytes 2359808 | tf_op jit(solution)/shard_map/sub | solution.py:685

commit v5 on v4

--- a/solution.py
+++ b/solution.py
@@ -30,8 +30,8 @@
     (0, 0, 1),
     (0, 0, -1),
 )
-UP = (2, 0, 4)
-DOWN = (3, 1, 5)
+UP = (0, 2, 4)
+DOWN = (1, 3, 5)
 LATE = (6, 7, 8, 9, 10, 11)
 FACES = ((1, 0, 0), (-1, 0, 0), (0, 1, 0), (0, -1, 0), (0, 0, 1), (0, 0, -1))
 START = (7, 6, 5, 4, 3, 2, 1, 0)
@@ -181,6 +181,8 @@
     ZR,
     DS,
     DR,
+    DX,
+    DXR,
     LOW,
     DN,
     MOM,
@@ -267,8 +269,8 @@
 
     def messages(j, which):
         pairs = (
-            (DS.at[j, 0], DR.at[j, 0]),
-            (DS.at[j, 1], DR.at[j, 1]),
+            (DX.at[j, 0], DXR.at[j, 0]),
+            (DX.at[j, 1], DXR.at[j, 1]),
             (DS.at[j, 2], DR.at[j, 2]),
             (DS.at[j, 3], DR.at[j, 3]),
             (F.at[j, 0:4, NB, BASE : BASE + ROWS], F.at[j, 0:4, 0, BASE : BASE + ROWS]),
@@ -303,10 +305,10 @@
 
     def diagonals(j, s0, s1, s2):
         if s0 is not None:
-            DS[j, 0] = jnp.broadcast_to(s0[0:1], (8, LANES))
+            DX[j, 0] = s0[0:1]
             DS[j, 2] = to_lanes(s0, 0)
         if s1 is not None:
-            DS[j, 1] = jnp.broadcast_to(s1[31:32], (8, LANES))
+            DX[j, 1] = s1[31:32]
             DS[j, 3] = to_lanes(s2, 127)
 
     slab = jnp.zeros((ROWS, LANES), F32)
@@ -365,7 +367,7 @@
         sub, lane8 = row_id(8), lane_id(8)
         s0, s1, s2, ph = YR[j, 0], YR[j, 1], YR[j, 2], YR[j, 3]
         own0, own2, own_ph = YS[j, 4], YS[j, 5], YS[j, 6]
-        s1x = jnp.where(sub == 7, DR[j, 1] if diag else 0.0, roll(s1, -1, 0))
+        s1x = jnp.where(sub == 7, DXR[j, 1] if diag else 0.0, roll(s1, -1, 0))
         s1z = jnp.where(lane8 == 127, roll(DR[j, 4], -1, 1), roll(s1, -1, 1))
         LOW[0] = CY[0] * ((own2 - s2) - (s1z - s1))
         LOW[1] = CY[1] * ((s1x - s1) - (own0 - s0))
@@ -415,7 +417,7 @@
         e0, e1, e2, ph = (field(j, f, -1) for f in range(4))
         n1, n2, nph = (field(j, f, 0) for f in (1, 2, 3))
         e0z = last_lane(from_lanes(DR[j, 2], 127) if diag else 0.0, roll(e0, -1, 1))
-        e0y = jnp.where(row_id() == 31, DR[j, 0, 0:1, :] if diag else 0.0, roll(e0, -1, 0))
+        e0y = jnp.where(row_id() == 31, DXR[j, 0] if diag else 0.0, roll(e0, -1, 0))
         g1 = CX[0] * ((e0z - e0) - (n2 - e2))
         g2 = CX[1] * ((n1 - e1) - (e0y - e0))
         return g1, g2, CX[2] * (e0 + (nph - ph))
@@ -493,9 +495,9 @@
         receive(j, (0, 1, 2, 3))
         end = NB - 1
         xz = jnp.where(lane_id() == 0, CZ7[...] * from_lanes(DR[j, 3], 0), 0.0)
-        xy = jnp.where(row_id() == 0, CY[1, end : end + 1, :] * DR[j, 1, 0:1, :], 0.0)
+        xy = jnp.where(row_id() == 0, CY[1, end : end + 1, :] * DXR[j, 1], 0.0)
         w0 = V[j + 1, 0, end] - scale * (xy + xz)
-        xy = jnp.where(row_id() == 31, CX[1, 31:32, :] * DR[j, 0, 0:1, :], 0.0)
+        xy = jnp.where(row_id() == 31, CX[1, 31:32, :] * DXR[j, 0], 0.0)
         w1 = V[j + 1, 1, 0] - scale * xy
         xz = jnp.where(lane_id() == 127, CX[0] * from_lanes(DR[j, 2], 127), 0.0)
         w2 = V[j + 1, 2, 0] - scale * xz
@@ -556,11 +558,13 @@
     SUM[0] = lanes_of(MOM[...])
     copies_0 = spread(0, group_a, 0, RA)
 
-    receive(last, (9, 11, 5))
+    receive(last, (9, 11))
     rows_above(last)
     high = ZR[last, 1]
     au = jnp.zeros((8, LANES), F32)
     for i in range(NB):
+        if i == NB - 1:
+            receive(last, (5,))
         ends = [roll(high, 127 - place(f, i) - 1, 1) for f in (0, 1, 3)]
         c, u = fluxes(last, i, ends)
         g = [K[n, i] * c[n] for n in range(3)]
@@ -663,6 +667,8 @@
             vm(4, 2, ROWS, LANES),
             vm(4, 4, 8, LANES),
             vm(4, 6, 8, LANES),
+            vm(4, 2, 1, LANES),
+            vm(4, 2, 1, LANES),
             vm(3, 8, LANES),
             vm(*shape[1:]),
             vm(8, LANES),

time: 39.2 us -> 39 us (level)
  no operation moved by 1% of the time
where the time goes in v5:
time: 39 us; the launch traced here: 38.9 us
  Pallas kernels  37.2 us (95%)
  other arithmetic  1.04 us (3%)
  between operations  0.64 us (2%)
    pallas_call x1, Pallas kernels, body(): pl.pallas_call(functools.partial(kernel, sizes), out_shape=(pltpu.VMEM(sh...  37.2 us
    sub x1, other arithmetic, body(): return (x + step * p, r - step * a)  1.04 us

profile of v5, /device:TPU:1, one launch (start us, length us, event | category | flops | bytes accessed | tf_op | source)
XLA Modules:
  0.0 38.9 jit_solution(3100321874106472271)
XLA Ops:
  0.6 37.2 %shard_map.50 = (f32[3,8,32,128]{3,2,1,0:T(8,128)S(1)}, f32[3,8,32,128]{3,2,1,0:T(8,128)S(1)}, f32[3,8,32,128]{3,2,1,0:T(8,128)S(1)}, f32[3,8,32,128]{3,2,1,0:T(8,128)S(1)}, f32[1,128]{1,0:T(1,128)S(1)}) custom-call(f32[3,8,32,128]{3,2,1,0:T(8,128)} %r_hbm.1, f32[3,8,32,128]{3,2,1,0:T(8,128)} %m_hbm.1, f32[3,8,32,128]{3,2,1,0:T(8,128)} %k_hbm.1), custom_call_target="tpu_custom_call" | custom-call | tf_op jit(solution)/shard_map/pallas_call | solution.py:640
  37.9 1.0 %multiply_subtract_fusion = (f32[3,8,32,128]{3,2,1,0:T(8,128)}, f32[3,8,32,128]{3,2,1,0:T(8,128)}) fusion(f32[3,8,32,128]{3,2,1,0:T(8,128)S(1)} %get-tuple-element.10, f32[3,8,32,128]{3,2,1,0:T(8,128)S(1)} %get-tuple-element.11, f32[128]{0:T(128)S(1)} %bitcast.1, f32[3,8,32,128]{3,2,1,0:T(8,128)S(1)} %get-tuple-element.7, f32[3,8,32,128]{3,2,1,0:T(8,128)S(1)} %get-tuple-element.9), kind=kLoop, calls=%fused_computation | loop fusion | flops 393216 | bytes 2359808 | tf_op jit(solution)/shard_map/sub | solution.py:691

commit v6 on v5

--- a/solution.py
+++ b/solution.py
@@ -32,7 +32,7 @@
 )
 UP = (0, 2, 4)
 DOWN = (1, 3, 5)
-LATE = (6, 7, 8, 9, 10, 11)
+LATE = (6, 7, 9, 11, 8, 10)
 FACES = ((1, 0, 0), (-1, 0, 0), (0, 1, 0), (0, -1, 0), (0, 0, 1), (0, 0, -1))
 START = (7, 6, 5, 4, 3, 2, 1, 0)
 
@@ -506,7 +506,7 @@
         send(j + 1, (0, 1, 2, 3))
         slab = finish(j + 1, end, slab, {0: s0})
         slab = finish(j + 1, 0, slab, {1: s1, 2: s2})
-        send(j + 1, (4, 5))
+        send(j + 1, (5, 4))
         V[j + 1, 0, end], V[j + 1, 1, 0], V[j + 1, 2, 0] = w0, w1, w2
         ZS[j + 1] = slab
         send(j + 1, LATE)
@@ -549,10 +549,19 @@
             c.start()
         return copies
 
-    def gather(n, copies, group, base, into):
-        for c in copies:
-            c.wait_recv()
-        return SUM[n] + jnp.sum(into[base : base + len(group)], axis=0)
+    def gather(n, copies, into):
+        total = SUM[n]
+        at = len(copies)
+        while at > 0:
+            low = max(0, at - 8)
+            for k in range(at - 1, low - 1, -1):
+                copies[k].wait_recv()
+            rows = [into[k] for k in range(low, at)]
+            while len(rows) > 1:
+                rows = [sum(rows[k + 1 : k + 2], rows[k]) for k in range(0, len(rows), 2)]
+            total = total + rows[0]
+            at = low
+        return total
 
     n_a, n_b = len(group_a), len(group_b)
     SUM[0] = lanes_of(MOM[...])
@@ -578,9 +587,9 @@
     au = jnp.sum(jnp.sum(au, axis=0, keepdims=True), axis=1, keepdims=True)
     SUM[1] = jnp.broadcast_to(au, (1, LANES))
     copies_1 = spread(1, pair, n_a + n_b, RC)
-    SUM[3] = gather(1, copies_1, pair, 0, RC)
+    SUM[3] = gather(1, copies_1, RC)
     copies_3 = spread(3, chips, n_a + n_b + 1, RD)
-    SUM[2] = gather(0, copies_0, group_a, 0, RA)
+    SUM[2] = gather(0, copies_0, RA)
     copies_2 = spread(2, group_b, n_a, RB)
     receive(last, (0, 1, 2, 3, 6, 7, 8, 10, 4))
     slabs = edges(last, True)
@@ -598,7 +607,7 @@
                 V[last + 1, n, i] = scale * w[n] - T[n, i]
 
     last_planes(range(0, NB))
-    total = gather(2, copies_2, group_b, 0, RB)
+    total = gather(2, copies_2, RB)
     moment = [
         jnp.broadcast_to(jnp.sum(jnp.where(lane_id(1) == m, total, 0.0), axis=1, keepdims=True), (1, LANES))
         for m in range(2 * ITERS - 1)
@@ -622,11 +631,29 @@
         return carry
 
     lax.fori_loop(0, ITERS, sent, 0)
-    for c in coef + copies_0 + copies_1 + copies_2 + copies_3:
+    for c in coef + copies_0 + copies_1 + copies_2:
         c.wait_send()
-    au = gather(3, copies_3, chips, 0, RD)
+    au = gather(3, copies_3, RD)
     top = scale * (au - THETA * moment[2 * last]) - moment[2 * last - 1]
     alpha_out[...] = gamma / (slack + weight * (2.0 * top - nu[1]))
+    for c in copies_3:
+        c.wait_send()
+
+
+def epilogue(x, p, r, a, alpha, x_out, r_out, X, R, sem):
+    step = alpha[...]
+    copies = []
+    for c in range(3):
+        for i in range(NB):
+            X[c, i] = x[c, i] + step * p[c, i]
+        copies.append(pltpu.make_async_copy(X.at[c], x_out.at[c], sem.at[2 * c]))
+        copies[-1].start()
+        for i in range(NB):
+            R[c, i] = r[c, i] - step * a[c, i]
+        copies.append(pltpu.make_async_copy(R.at[c], r_out.at[c], sem.at[2 * c + 1]))
+        copies[-1].start()
+    for c in copies:
+        c.wait()
 
 
 def body(sizes, right_side, mass_coef, curl_coef):
@@ -687,8 +714,14 @@
         ],
         compiler_params=pltpu.CompilerParams(collective_id=0, has_side_effects=True),
     )(right_side, mass_coef, curl_coef)
-    step = jnp.broadcast_to(alpha[0], shape)
-    return x + step * p, r - step * a
+    return pl.pallas_call(
+        epilogue,
+        out_shape=(jax.ShapeDtypeStruct(shape, F32),) * 2,
+        in_specs=[pl.BlockSpec(memory_space=pltpu.VMEM)] * 5,
+        out_specs=[pl.BlockSpec(memory_space=pl.ANY)] * 2,
+        scratch_shapes=[vm(*shape), vm(*shape), dma(6)],
+        compiler_params=pltpu.CompilerParams(vmem_limit_bytes=2 << 20),
+    )(x, p, r, a, alpha)
 
 
 def solution(mesh):

time: 39 us -> 39 us (level)
  other arithmetic: 1.04 us -> 0 us
  Pallas kernels: 37.2 us -> 38.2 us
    sub x1 -> x0, other arithmetic: 1.04 us -> none  [body(): return (x + step * p, r - step * a)]
    pallas_call x0 -> x1, Pallas kernels: none -> 0.94 us  [body(): pl.pallas_call(epilogue, out_shape=(jax.ShapeDtypeStruct(shape, F32),) *...]
where the time goes in v6:
time: 39 us; the launch traced here: 38.8 us
  Pallas kernels  38.2 us (98%)
  between operations  0.64 us (2%)
    pallas_call x1, Pallas kernels, body(): pl.pallas_call(functools.partial(kernel, sizes), out_shape=(pltpu.VMEM(sh...  37.2 us
    pallas_call x1, Pallas kernels, body(): pl.pallas_call(epilogue, out_shape=(jax.ShapeDtypeStruct(shape, F32),) *...  0.94 us

profile of v6, /device:TPU:1, one launch (start us, length us, event | category | flops | bytes accessed | tf_op | source)
XLA Modules:
  0.0 38.8 jit_solution(5726233864068565343)
XLA Ops:
  0.6 37.2 %shard_map.50 = (f32[3,8,32,128]{3,2,1,0:T(8,128)S(1)}, f32[3,8,32,128]{3,2,1,0:T(8,128)S(1)}, f32[3,8,32,128]{3,2,1,0:T(8,128)S(1)}, f32[3,8,32,128]{3,2,1,0:T(8,128)S(1)}, f32[1,128]{1,0:T(1,128)S(1)}) custom-call(f32[3,8,32,128]{3,2,1,0:T(8,128)} %r_hbm.1, f32[3,8,32,128]{3,2,1,0:T(8,128)} %m_hbm.1, f32[3,8,32,128]{3,2,1,0:T(8,128)} %k_hbm.1), custom_call_target="tpu_custom_call" | custom-call | tf_op jit(solution)/shard_map/pallas_call | solution.py:667
  37.9 0.9 %shard_map.51 = (f32[3,8,32,128]{3,2,1,0:T(8,128)}, f32[3,8,32,128]{3,2,1,0:T(8,128)}) custom-call(f32[3,8,32,128]{3,2,1,0:T(8,128)S(1)} %get-tuple-element.7.x, f32[3,8,32,128]{3,2,1,0:T(8,128)S(1)} %get-tuple-element.8.p, f32[3,8,32,128]{3,2,1,0:T(8,128)S(1)} %get-tuple-element.9.r, f32[3,8,32,128]{3,2,1,0:T(8,128)S(1)} %get-tuple-element.10.a, ...), custom_call_target="tpu_custom_call" | custom-call | tf_op jit(solution)/shard_map/pallas_call | solution.py:717
